TPU v7x, 128 devices: a whole 4x4x4 slice. The times are simulated.
128 devices in a mesh: section: 8 (over y, core), dp: 16 (over z, x).
Axes of the slice: x: 4, y: 4, z: 4, core: 2. Of those that a mesh axis runs over, the one named last changes fastest.
Arguments:
- acts: bfloat16 [8, 8192, 3584], P('section', 'dp'), may hold values from -400 to 400
- cotangent: bfloat16 [8192, 3584], P('dp'), may hold values from -6 to 6
- frozen: bfloat16 [8, 3584, 3584], P('section', 'dp'), may hold values from -0.09375 to 0.09375
- down_adapter: bfloat16 [8, 16, 3584], P('section'), may hold values from -0.25 to 0.25
- up_adapter: bfloat16 [8, 16, 3584], P('section'), may hold values from -0.25 to 0.25
- example_ids: int32 [16, 4], P('dp'), may hold values from 0 to 3, each once within a row
- lengths: int32 [16, 4], P('dp'), may hold values from 32 to 128
Outputs:
- grad_down: float32 [8, 16, 3584], P('section', None, 'dp')
- grad_up: float32 [8, 16, 3584], P('section', None, 'dp')
- example_norms: float32 [16, 4], P('dp')
Inputs may be any that keep to these rules, and one draw needn't show every extreme that they name: `example_ids`: each row is an ordering of the 4 examples of one replica.
All inputs are finite; a program needn't handle non-finite values.
Results may differ from a plain program's by a relative error of at most 0.009.
Values may be sent and summed in bfloat16 or wider, within the bound.
A program may use at most 128 MiB of HBM per device.

v0:
```python
import math

import jax
import jax.numpy as jnp
from jax import lax
from jax.sharding import PartitionSpec as P


def from_behind(value, axis, steps):
    count = lax.axis_size(axis)
    first, last = (max(0, -steps), min(count, count - steps))
    return lax.ppermute(value, axis, [(source, source + steps) for source in range(first, last)])


def sent_to_all(value, axis):
    size = lax.axis_size(axis)
    return lax.all_to_all(
        jnp.broadcast_to(value[None], (size, *value.shape)), axis, 0, 0, tiled=True
    )


def taken_together(value, axis):
    return sent_to_all(value, axis).sum(axis=0)


def split_up(value, dim, size):
    shape = value.shape
    pieces = value.reshape(*shape[:dim], size, shape[dim] // size, *shape[dim + 1 :])
    return jnp.moveaxis(pieces, dim, 0)


def sent_and_summed(value, axis, dim):
    pieces = split_up(value, dim, lax.axis_size(axis))
    arrived = lax.all_to_all(pieces, axis, split_axis=0, concat_axis=0, tiled=True)
    return arrived.sum(axis=0)


def side_by_side(arrays, axis, dim, along):
    ends, at = ([], 0)
    for a in arrays[:-1]:
        at += a.shape[along]
        ends.append(at)
    both = jnp.concatenate(arrays, axis=along)
    return tuple(jnp.split(sent_and_summed(both, axis, dim), ends, axis=along))


def on_device(acts, cotangent, frozen, down_adapter, up_adapter, example_ids, lengths):
    section_count = lax.axis_size("section")
    section_index = lax.axis_index("section")
    replica_count = lax.axis_size("dp")
    layer_inputs = acts[0]
    down_rows = down_adapter[0]
    up_rows = up_adapter[0]
    slot_count = example_ids.shape[1]
    positions = layer_inputs.shape[0] // slot_count
    features = layer_inputs.shape[1]
    rank_size = down_rows.shape[0]
    choose = (example_ids[0][:, None] == jnp.arange(slot_count, dtype=jnp.int32)[None, :]).astype(
        jnp.int32
    )
    slot_length = jnp.sum(choose * lengths[0][None, :], axis=1)
    live_mask = (jnp.arange(positions, dtype=jnp.int32)[None, :] < slot_length[:, None]).astype(
        jnp.bfloat16
    )
    seeded = cotangent.reshape(slot_count, positions, features) * live_mask[:, :, None]
    input_blocks = layer_inputs.reshape(slot_count, positions, features)
    clip_scale = math.sqrt(2.0 * rank_size * features) / math.sqrt(replica_count * slot_count)
    weight = lax.all_gather(frozen[0], "dp", axis=0, tiled=True)

    def backstep(out_grad):
        up_grad = jnp.dot(out_grad, up_rows.T, preferred_element_type=jnp.float32).astype(
            jnp.bfloat16
        )
        in_grad = jnp.dot(out_grad, weight.T, preferred_element_type=jnp.float32)
        in_grad = in_grad + jnp.dot(up_grad, down_rows, preferred_element_type=jnp.float32)
        return in_grad.astype(jnp.bfloat16)

    def local_terms(out_grad, inputs):
        up_grad = jnp.dot(out_grad, up_rows.T, preferred_element_type=jnp.float32).astype(
            jnp.bfloat16
        )
        down_act = jnp.dot(inputs, down_rows.T, preferred_element_type=jnp.float32).astype(
            jnp.bfloat16
        )
        down_term = jnp.dot(up_grad.T, inputs, preferred_element_type=jnp.float32)
        up_term = jnp.dot(down_act.T, out_grad, preferred_element_type=jnp.float32)
        square_sum = jnp.sum(down_term * down_term) + jnp.sum(up_term * up_term)
        return (square_sum, down_term, up_term)

    tick_count = slot_count + section_count - 1
    incoming = jnp.zeros((positions, features), jnp.bfloat16)
    stored_grads = jnp.zeros((slot_count, positions, features), jnp.bfloat16)
    sum_down = jnp.zeros((rank_size, features), jnp.float32)
    sum_up = jnp.zeros((rank_size, features), jnp.float32)
    slot_norms = jnp.zeros((slot_count,), jnp.float32)

    def tick_step(tick, carry):
        incoming, stored_grads, sum_down, sum_up, slot_norms = carry
        micro_index = tick - (section_count - 1 - section_index)
        active = (micro_index >= 0) & (micro_index < slot_count)
        held_index = jnp.clip(micro_index, 0, slot_count - 1)
        fresh = lax.dynamic_index_in_dim(seeded, held_index, 0, keepdims=False)
        start = jnp.where(section_index == section_count - 1, fresh, incoming)
        produced = lax.cond(active, backstep, lambda value: jnp.zeros_like(value), start)
        previous = lax.dynamic_index_in_dim(stored_grads, held_index, 0, keepdims=False)
        kept = jnp.where(active, start, previous)
        stored_grads = lax.dynamic_update_index_in_dim(stored_grads, kept, held_index, 0)
        incoming = from_behind(produced, "section", -1)
        return (incoming, stored_grads, sum_down, sum_up, slot_norms)

    carry = (incoming, stored_grads, sum_down, sum_up, slot_norms)
    incoming, stored_grads, sum_down, sum_up, slot_norms = lax.fori_loop(
        0, tick_count, tick_step, carry
    )
    square_sums, down_terms, up_terms = jax.vmap(local_terms)(stored_grads, input_blocks)
    totals = taken_together(square_sums, "section")
    slot_norms = jnp.sqrt(totals)
    factors = clip_scale / (slot_norms + 0.01)
    sum_down = jnp.sum(factors[:, None, None] * down_terms, axis=0)
    sum_up = jnp.sum(factors[:, None, None] * up_terms, axis=0)
    grad_down, grad_up = side_by_side((sum_down, sum_up), "dp", 1, 0)
    example_norms = jnp.sum(choose.astype(jnp.float32) * slot_norms[:, None], axis=0)
    return (grad_down[None], grad_up[None], example_norms[None])


def solution(mesh):
    in_specs = (
        P("section", "dp", None),
        P("dp", None),
        P("section", "dp", None),
        P("section", None, None),
        P("section", None, None),
        P("dp", None),
        P("dp", None),
    )
    out_specs = (P("section", None, "dp"), P("section", None, "dp"), P("dp", None))
    return jax.shard_map(
        on_device, mesh=mesh, in_specs=in_specs, out_specs=out_specs, check_vma=False
    )
```

profile of v0, /device:TPU:1, one launch (start us, length us, event | category | flops | bytes accessed | tf_op | source)
XLA Modules:
  0.0 537.3 jit_solution(118021196939126210)
XLA Ops:
  13.0 157.1 %all-gather.3.cloned.1.call-done = bf16[1,3584,3584]{2,1,0:T(8,128)(2,1)} async-done(((bf16[1,224,3584]{2,1,0:T(8,128)(2,1)}), bf16[1,3584,3584]{2,1,0:T(8,128)(2,1)}) %all-gather.3.cloned.1.call-update) | async-done | bytes 25690128 | tf_op jit(solution)/shard_map/all_gather | solution.py:68
  172.3 324.4 %while.17 = (s32[]{:T(128)}, bf16[128,3584]{1,0:T(8,128)(2,1)S(1)}, bf16[4,128,3584]{2,1,0:T(8,128)(2,1)}, s32[]{:T(128)}, pred[]{:T(512)}, /*index=5*/bf16[4,12...) while((s32[]{:T(128)}, bf16[128,3584]{1,0:T(8,128)(2,1)S(1)}, ...), condition=%wide.region_4.5_spmd, body=%wide.region_1.4_spmd.sunk | while | flops 3319531520 | bytes 42435348 | solution.py:112
  179.9 12.4 %collective-permute-done = bf16[128,3584]{1,0:T(8,128)(2,1)S(1)} collective-permute-done((bf16[128,3584]{1,0:T(8,128)(2,1)}, bf16[128,3584]{1,0:T(8,128)(2,1)S(1)}, u32[]{:S(2)}, u32[]{:S(2)}) %collective-permute-start) | collective-permute-done | bytes 917536 | tf_op jit(solution)/shard_map/while/body/eval_jaxpr/ppermute | solution.py:12
  199.1 13.0 %collective-permute-done = bf16[128,3584]{1,0:T(8,128)(2,1)S(1)} collective-permute-done((bf16[128,3584]{1,0:T(8,128)(2,1)}, bf16[128,3584]{1,0:T(8,128)(2,1)S(1)}, u32[]{:S(2)}, u32[]{:S(2)}) %collective-permute-start) | collective-permute-done | bytes 917536 | tf_op jit(solution)/shard_map/while/body/eval_jaxpr/ppermute | solution.py:12
  218.9 13.0 %collective-permute-done = bf16[128,3584]{1,0:T(8,128)(2,1)S(1)} collective-permute-done((bf16[128,3584]{1,0:T(8,128)(2,1)}, bf16[128,3584]{1,0:T(8,128)(2,1)S(1)}, u32[]{:S(2)}, u32[]{:S(2)}) %collective-permute-start) | collective-permute-done | bytes 917536 | tf_op jit(solution)/shard_map/while/body/eval_jaxpr/ppermute | solution.py:12
  238.7 13.0 %collective-permute-done = bf16[128,3584]{1,0:T(8,128)(2,1)S(1)} collective-permute-done((bf16[128,3584]{1,0:T(8,128)(2,1)}, bf16[128,3584]{1,0:T(8,128)(2,1)S(1)}, u32[]{:S(2)}, u32[]{:S(2)}) %collective-permute-start) | collective-permute-done | bytes 917536 | tf_op jit(solution)/shard_map/while/body/eval_jaxpr/ppermute | solution.py:12
  258.5 13.0 %collective-permute-done = bf16[128,3584]{1,0:T(8,128)(2,1)S(1)} collective-permute-done((bf16[128,3584]{1,0:T(8,128)(2,1)}, bf16[128,3584]{1,0:T(8,128)(2,1)S(1)}, u32[]{:S(2)}, u32[]{:S(2)}) %collective-permute-start) | collective-permute-done | bytes 917536 | tf_op jit(solution)/shard_map/while/body/eval_jaxpr/ppermute | solution.py:12
  278.3 63.4 %collective-permute-done = bf16[128,3584]{1,0:T(8,128)(2,1)S(1)} collective-permute-done((bf16[128,3584]{1,0:T(8,128)(2,1)}, bf16[128,3584]{1,0:T(8,128)(2,1)S(1)}, u32[]{:S(2)}, u32[]{:S(2)}) %collective-permute-start) | collective-permute-done | bytes 917536 | tf_op jit(solution)/shard_map/while/body/eval_jaxpr/ppermute | solution.py:12
  345.5 15.1 %conditional.2 = (bf16[128,3584]{1,0:T(8,128)(2,1)}) conditional(s32[]{:T(128)} %convert_element_type.57, () %tuple.55, (bf16[128,3584]{1,0:T(8,128)(2,1)S(1)}, bf16[3584,3584]{1,0:T(8,128)(2,1)}, bf16[16,3584]{1,0:T(8,128)(2,1)S(1)}, bf16[16,3584]{1,0:T(8,128)(2,1)S(1)}) %tuple.56), branch_computations={%region_2.2_spmd, %region_3.3_spmd} | conditional | flops 3318614016 | bytes 32342024 | solution.py:104
  345.5 12.9 %fusion.13 = f32[128,3584]{1,0:T(8,128)S(1)} fusion(bf16[128,3584]{1,0:T(8,128)(2,1)S(1)} %get-tuple-element.202, bf16[3584,3584]{1,0:T(8,128)(2,1)} %get-tuple-element.203), kind=kOutput, calls=%fused_computation.28 | convolution fusion | flops 3288334336 | bytes 28442624 | tf_op jit(solution)/shard_map/while/body/eval_jaxpr/cond/branch_1_fun/dot_general | solution.py:74
  362.5 13.0 %collective-permute-done = bf16[128,3584]{1,0:T(8,128)(2,1)S(1)} collective-permute-done((bf16[128,3584]{1,0:T(8,128)(2,1)}, bf16[128,3584]{1,0:T(8,128)(2,1)S(1)}, u32[]{:S(2)}, u32[]{:S(2)}) %collective-permute-start) | collective-permute-done | bytes 917536 | tf_op jit(solution)/shard_map/while/body/eval_jaxpr/ppermute | solution.py:12
  379.3 15.1 %conditional.2 = (bf16[128,3584]{1,0:T(8,128)(2,1)}) conditional(s32[]{:T(128)} %convert_element_type.57, () %tuple.55, (bf16[128,3584]{1,0:T(8,128)(2,1)S(1)}, bf16[3584,3584]{1,0:T(8,128)(2,1)}, bf16[16,3584]{1,0:T(8,128)(2,1)S(1)}, bf16[16,3584]{1,0:T(8,128)(2,1)S(1)}) %tuple.56), branch_computations={%region_2.2_spmd, %region_3.3_spmd} | conditional | flops 3318614016 | bytes 32342024 | solution.py:104
  379.3 12.9 %fusion.13 = f32[128,3584]{1,0:T(8,128)S(1)} fusion(bf16[128,3584]{1,0:T(8,128)(2,1)S(1)} %get-tuple-element.202, bf16[3584,3584]{1,0:T(8,128)(2,1)} %get-tuple-element.203), kind=kOutput, calls=%fused_computation.28 | convolution fusion | flops 3288334336 | bytes 28442624 | tf_op jit(solution)/shard_map/while/body/eval_jaxpr/cond/branch_1_fun/dot_general | solution.py:74
  396.3 13.0 %collective-permute-done = bf16[128,3584]{1,0:T(8,128)(2,1)S(1)} collective-permute-done((bf16[128,3584]{1,0:T(8,128)(2,1)}, bf16[128,3584]{1,0:T(8,128)(2,1)S(1)}, u32[]{:S(2)}, u32[]{:S(2)}) %collective-permute-start) | collective-permute-done | bytes 917536 | tf_op jit(solution)/shard_map/while/body/eval_jaxpr/ppermute | solution.py:12
  413.1 15.1 %conditional.2 = (bf16[128,3584]{1,0:T(8,128)(2,1)}) conditional(s32[]{:T(128)} %convert_element_type.57, () %tuple.55, (bf16[128,3584]{1,0:T(8,128)(2,1)S(1)}, bf16[3584,3584]{1,0:T(8,128)(2,1)}, bf16[16,3584]{1,0:T(8,128)(2,1)S(1)}, bf16[16,3584]{1,0:T(8,128)(2,1)S(1)}) %tuple.56), branch_computations={%region_2.2_spmd, %region_3.3_spmd} | conditional | flops 3318614016 | bytes 32342024 | solution.py:104
  413.1 12.9 %fusion.13 = f32[128,3584]{1,0:T(8,128)S(1)} fusion(bf16[128,3584]{1,0:T(8,128)(2,1)S(1)} %get-tuple-element.202, bf16[3584,3584]{1,0:T(8,128)(2,1)} %get-tuple-element.203), kind=kOutput, calls=%fused_computation.28 | convolution fusion | flops 3288334336 | bytes 28442624 | tf_op jit(solution)/shard_map/while/body/eval_jaxpr/cond/branch_1_fun/dot_general | solution.py:74
  430.1 13.0 %collective-permute-done = bf16[128,3584]{1,0:T(8,128)(2,1)S(1)} collective-permute-done((bf16[128,3584]{1,0:T(8,128)(2,1)}, bf16[128,3584]{1,0:T(8,128)(2,1)S(1)}, u32[]{:S(2)}, u32[]{:S(2)}) %collective-permute-start) | collective-permute-done | bytes 917536 | tf_op jit(solution)/shard_map/while/body/eval_jaxpr/ppermute | solution.py:12
  446.9 15.1 %conditional.2 = (bf16[128,3584]{1,0:T(8,128)(2,1)}) conditional(s32[]{:T(128)} %convert_element_type.57, () %tuple.55, (bf16[128,3584]{1,0:T(8,128)(2,1)S(1)}, bf16[3584,3584]{1,0:T(8,128)(2,1)}, bf16[16,3584]{1,0:T(8,128)(2,1)S(1)}, bf16[16,3584]{1,0:T(8,128)(2,1)S(1)}) %tuple.56), branch_computations={%region_2.2_spmd, %region_3.3_spmd} | conditional | flops 3318614016 | bytes 32342024 | solution.py:104
  446.9 12.9 %fusion.13 = f32[128,3584]{1,0:T(8,128)S(1)} fusion(bf16[128,3584]{1,0:T(8,128)(2,1)S(1)} %get-tuple-element.202, bf16[3584,3584]{1,0:T(8,128)(2,1)} %get-tuple-element.203), kind=kOutput, calls=%fused_computation.28 | convolution fusion | flops 3288334336 | bytes 28442624 | tf_op jit(solution)/shard_map/while/body/eval_jaxpr/cond/branch_1_fun/dot_general | solution.py:74
  463.9 13.0 %collective-permute-done = bf16[128,3584]{1,0:T(8,128)(2,1)S(1)} collective-permute-done((bf16[128,3584]{1,0:T(8,128)(2,1)}, bf16[128,3584]{1,0:T(8,128)(2,1)S(1)}, u32[]{:S(2)}, u32[]{:S(2)}) %collective-permute-start) | collective-permute-done | bytes 917536 | tf_op jit(solution)/shard_map/while/body/eval_jaxpr/ppermute | solution.py:12
  481.7 5.6 %collective-permute-start = (bf16[128,3584]{1,0:T(8,128)(2,1)}, bf16[128,3584]{1,0:T(8,128)(2,1)S(1)}, u32[]{:S(2)}, u32[]{:S(2)}) collective-permute-start(bf16[128,3584]{1,0:T(8,128)(2,1)} %get-tuple-element.349), channel_id=1, source_target_pairs={{16,0},{32,16},{48,32},{64,48},{80,64},{96,80},{112,96},{17,1},{33... | collective-permute-start | bytes 2752520 | tf_op jit(solution)/shard_map/while/body/eval_jaxpr/ppermute | solution.py:12
  487.4 9.3 %collective-permute-done = bf16[128,3584]{1,0:T(8,128)(2,1)S(1)} collective-permute-done((bf16[128,3584]{1,0:T(8,128)(2,1)}, bf16[128,3584]{1,0:T(8,128)(2,1)S(1)}, u32[]{:S(2)}, u32[]{:S(2)}) %collective-permute-start) | collective-permute-done | bytes 917536 | tf_op jit(solution)/shard_map/while/body/eval_jaxpr/ppermute | solution.py:12
  506.4 6.2 %all_to_all.11 = f32[8,1,4]{2,1,0:T(1,128)S(1)} all-to-all(f32[8,1,4]{2,1,0:T(1,128)S(1)} %broadcast_in_dim.36), channel_id=1, replica_groups=mesh['section'=8,'dp'=16] {'section'}, dimensions={0} | all-to-all | bytes 256 | tf_op jit(solution)/shard_map/all_to_all | solution.py:17
  520.0 9.8 %all-to-all-done.1 = f32[16,32,224]{2,1,0:T(8,128)S(1)} async-done(((f32[16,32,224]{2,1,0:T(8,128)}), f32[16,32,224]{2,1,0:T(8,128)S(1)}, u32[]{:S(2)}, u32[]{:S(2)}) %all-to-all-start.1) | async-done | bytes 458784 | tf_op jit(solution)/shard_map/all_to_all | solution.py:34
  (77 shorter events, 110.8 us)
Async XLA Ops:
  7.2 162.9 %all-gather.3.cloned.1.call-start = ((), (), s32[]{:S(2)}) async-start(), calls=%async_computation.2 | async-start | bytes 27295744 | tf_op jit(solution)/shard_map/all_gather | solution.py:68
  13.0 159.3 %copy-start = (bf16[1,16,3584]{2,1,0:T(8,128)(2,1)S(1)}, bf16[1,16,3584]{2,1,0:T(8,128)(2,1)}, u32[]{:S(2)}) copy-start(bf16[1,16,3584]{2,1,0:T(8,128)(2,1)} %param.15) | copy-start | bytes 344068
  13.0 159.3 %copy-start.1 = (bf16[1,16,3584]{2,1,0:T(8,128)(2,1)S(1)}, bf16[1,16,3584]{2,1,0:T(8,128)(2,1)}, u32[]{:S(2)}) copy-start(bf16[1,16,3584]{2,1,0:T(8,128)(2,1)} %param.14) | copy-start | bytes 344068
  177.2 15.1 %collective-permute-start = (bf16[128,3584]{1,0:T(8,128)(2,1)}, bf16[128,3584]{1,0:T(8,128)(2,1)S(1)}, u32[]{:S(2)}, u32[]{:S(2)}) collective-permute-start(bf16[128,3584]{1,0:T(8,128)(2,1)} %get-tuple-element.349), channel_id=1, source_target_pairs={{16,0},{32,16},{48,32},{64,48},{80,64},{96,80},{112,96},{17,1},{33... | collective-permute-start | bytes 2752520 | tf_op jit(solution)/shard_map/while/body/eval_jaxpr/ppermute | solution.py:12
  197.2 14.9 %collective-permute-start = (bf16[128,3584]{1,0:T(8,128)(2,1)}, bf16[128,3584]{1,0:T(8,128)(2,1)S(1)}, u32[]{:S(2)}, u32[]{:S(2)}) collective-permute-start(bf16[128,3584]{1,0:T(8,128)(2,1)} %get-tuple-element.349), channel_id=1, source_target_pairs={{16,0},{32,16},{48,32},{64,48},{80,64},{96,80},{112,96},{17,1},{33... | collective-permute-start | bytes 2752520 | tf_op jit(solution)/shard_map/while/body/eval_jaxpr/ppermute | solution.py:12
  217.0 14.9 %collective-permute-start = (bf16[128,3584]{1,0:T(8,128)(2,1)}, bf16[128,3584]{1,0:T(8,128)(2,1)S(1)}, u32[]{:S(2)}, u32[]{:S(2)}) collective-permute-start(bf16[128,3584]{1,0:T(8,128)(2,1)} %get-tuple-element.349), channel_id=1, source_target_pairs={{16,0},{32,16},{48,32},{64,48},{80,64},{96,80},{112,96},{17,1},{33... | collective-permute-start | bytes 2752520 | tf_op jit(solution)/shard_map/while/body/eval_jaxpr/ppermute | solution.py:12
  236.7 14.9 %collective-permute-start = (bf16[128,3584]{1,0:T(8,128)(2,1)}, bf16[128,3584]{1,0:T(8,128)(2,1)S(1)}, u32[]{:S(2)}, u32[]{:S(2)}) collective-permute-start(bf16[128,3584]{1,0:T(8,128)(2,1)} %get-tuple-element.349), channel_id=1, source_target_pairs={{16,0},{32,16},{48,32},{64,48},{80,64},{96,80},{112,96},{17,1},{33... | collective-permute-start | bytes 2752520 | tf_op jit(solution)/shard_map/while/body/eval_jaxpr/ppermute | solution.py:12
  256.5 14.9 %collective-permute-start = (bf16[128,3584]{1,0:T(8,128)(2,1)}, bf16[128,3584]{1,0:T(8,128)(2,1)S(1)}, u32[]{:S(2)}, u32[]{:S(2)}) collective-permute-start(bf16[128,3584]{1,0:T(8,128)(2,1)} %get-tuple-element.349), channel_id=1, source_target_pairs={{16,0},{32,16},{48,32},{64,48},{80,64},{96,80},{112,96},{17,1},{33... | collective-permute-start | bytes 2752520 | tf_op jit(solution)/shard_map/while/body/eval_jaxpr/ppermute | solution.py:12
  276.3 65.3 %collective-permute-start = (bf16[128,3584]{1,0:T(8,128)(2,1)}, bf16[128,3584]{1,0:T(8,128)(2,1)S(1)}, u32[]{:S(2)}, u32[]{:S(2)}) collective-permute-start(bf16[128,3584]{1,0:T(8,128)(2,1)} %get-tuple-element.349), channel_id=1, source_target_pairs={{16,0},{32,16},{48,32},{64,48},{80,64},{96,80},{112,96},{17,1},{33... | collective-permute-start | bytes 2752520 | tf_op jit(solution)/shard_map/while/body/eval_jaxpr/ppermute | solution.py:12
  360.6 14.9 %collective-permute-start = (bf16[128,3584]{1,0:T(8,128)(2,1)}, bf16[128,3584]{1,0:T(8,128)(2,1)S(1)}, u32[]{:S(2)}, u32[]{:S(2)}) collective-permute-start(bf16[128,3584]{1,0:T(8,128)(2,1)} %get-tuple-element.349), channel_id=1, source_target_pairs={{16,0},{32,16},{48,32},{64,48},{80,64},{96,80},{112,96},{17,1},{33... | collective-permute-start | bytes 2752520 | tf_op jit(solution)/shard_map/while/body/eval_jaxpr/ppermute | solution.py:12
  394.4 14.9 %collective-permute-start = (bf16[128,3584]{1,0:T(8,128)(2,1)}, bf16[128,3584]{1,0:T(8,128)(2,1)S(1)}, u32[]{:S(2)}, u32[]{:S(2)}) collective-permute-start(bf16[128,3584]{1,0:T(8,128)(2,1)} %get-tuple-element.349), channel_id=1, source_target_pairs={{16,0},{32,16},{48,32},{64,48},{80,64},{96,80},{112,96},{17,1},{33... | collective-permute-start | bytes 2752520 | tf_op jit(solution)/shard_map/while/body/eval_jaxpr/ppermute | solution.py:12
  428.2 14.9 %collective-permute-start = (bf16[128,3584]{1,0:T(8,128)(2,1)}, bf16[128,3584]{1,0:T(8,128)(2,1)S(1)}, u32[]{:S(2)}, u32[]{:S(2)}) collective-permute-start(bf16[128,3584]{1,0:T(8,128)(2,1)} %get-tuple-element.349), channel_id=1, source_target_pairs={{16,0},{32,16},{48,32},{64,48},{80,64},{96,80},{112,96},{17,1},{33... | collective-permute-start | bytes 2752520 | tf_op jit(solution)/shard_map/while/body/eval_jaxpr/ppermute | solution.py:12
  462.0 14.9 %collective-permute-start = (bf16[128,3584]{1,0:T(8,128)(2,1)}, bf16[128,3584]{1,0:T(8,128)(2,1)S(1)}, u32[]{:S(2)}, u32[]{:S(2)}) collective-permute-start(bf16[128,3584]{1,0:T(8,128)(2,1)} %get-tuple-element.349), channel_id=1, source_target_pairs={{16,0},{32,16},{48,32},{64,48},{80,64},{96,80},{112,96},{17,1},{33... | collective-permute-start | bytes 2752520 | tf_op jit(solution)/shard_map/while/body/eval_jaxpr/ppermute | solution.py:12
  481.7 14.9 %collective-permute-start = (bf16[128,3584]{1,0:T(8,128)(2,1)}, bf16[128,3584]{1,0:T(8,128)(2,1)S(1)}, u32[]{:S(2)}, u32[]{:S(2)}) collective-permute-start(bf16[128,3584]{1,0:T(8,128)(2,1)} %get-tuple-element.349), channel_id=1, source_target_pairs={{16,0},{32,16},{48,32},{64,48},{80,64},{96,80},{112,96},{17,1},{33... | collective-permute-start | bytes 2752520 | tf_op jit(solution)/shard_map/while/body/eval_jaxpr/ppermute | solution.py:12
  506.4 12.9 %copy-start.2 = (s32[1,4]{1,0:T(1,128)S(1)}, s32[1,4]{1,0:T(1,128)}, u32[]{:S(2)}) copy-start(s32[1,4]{1,0:T(1,128)} %param.16) | copy-start | bytes 52
  514.4 15.4 %all-to-all-start.1 = ((f32[16,32,224]{2,1,0:T(8,128)}), f32[16,32,224]{2,1,0:T(8,128)S(1)}, u32[]{:S(2)}, u32[]{:S(2)}) async-start(f32[16,32,224]{2,1,0:T(8,128)} %copy.13), calls=%async_computation.1 | async-start | bytes 1048576 | tf_op jit(solution)/shard_map/all_to_all | solution.py:34
Sparse Core Ops, SparseCore 0:
  10.1 159.9 all-gather.2
where the time goes:
time: 539 us; the launch traced here: 537 us
  waiting for transfers between devices  357 us (66%)
  matrix products  70.1 us (13%)
  other arithmetic  34.6 us (6%)
  starting transfers between devices  30.6 us (6%)
  local copies, waits for them, and re-layouts  25 us (5%)
  between operations  14.1 us (3%)
  blocking collectives  6.18 us (1%)
    ppermute x11, waiting for transfers between devices, from_behind(): lax.ppermute(value, axis, [(source, source + steps) for source in range(f...  189 us
    all_gather x1, waiting for transfers between devices, on_device(): weight = lax.all_gather(frozen[0], 'dp', axis=0, tiled=True)  157 us
    dot_general x4, matrix products, backstep(): in_grad = jnp.dot(out_grad, weight.T, preferred_element_type=jnp.float32)  51.6 us
    dynamic_update_slice x11, other arithmetic, tick_step(): lax.dynamic_update_index_in_dim(stored_grads, kept, held_index, 0)  28.6 us
    ppermute x11, starting transfers between devices, from_behind(): lax.ppermute(value, axis, [(source, source + steps) for source in range(f...  25.5 us
    dynamic_slice x11, local copies, waits for them, and re-layouts, tick_step(): lax.dynamic_index_in_dim(stored_grads, held_index, 0, keepdims=False)  13.6 us
  transfers between devices with their start and end apart: 13, of which 13 were waited for; matrix products, arithmetic and copies ran while one was open for 1% of the time, Pallas kernels for 0%

commit v1 on v0

v1 whole, which is shorter than its diff:
```python
import functools
import math

import jax
import jax.numpy as jnp
from jax import lax
from jax.experimental import pallas as pl
from jax.experimental.pallas import tpu as pltpu
from jax.sharding import PartitionSpec as P

MESH = pl.DeviceIdType.MESH
NT = (((1,), (1,)), ((), ()))
CHUNKS = 7
LANES = 128


def fdot(a, b, dims=None):
    if dims is None:
        return jnp.dot(a, b, preferred_element_type=jnp.float32)
    return lax.dot_general(a, b, dims, preferred_element_type=jnp.float32)


def kernel(
    sections, replicas, clip_scale,
    w_hbm, seed_hbm, acts_hbm, up_ref, down_ref, downt_ref,
    red_ref, norm_ref,
    wbuf, gbuf, obuf, abuf, ugbuf, dabuf, tbuf, sqbuf, sqall, redsend, redin,
    w_sem, seed_sem, a_sem, send_sem, recv_sem, sqs_sem, sqr_sem, rs_sem, rr_sem,
):
    s = lax.axis_index("section")
    d = lax.axis_index("dp")
    slots, features, tokens = gbuf.shape
    rank = up_ref.shape[0]
    rows = features // CHUNKS
    span = features // replicas
    window = redin.shape[2]

    barrier = pltpu.get_barrier_semaphore()
    for k in range(1, sections):
        pl.semaphore_signal(barrier, inc=1, device_id=((s + k) % sections, d), device_id_type=MESH)
    for k in range(1, replicas):
        pl.semaphore_signal(barrier, inc=1, device_id=(s, (d + k) % replicas), device_id_type=MESH)

    def w_copy(c):
        at = pl.ds(c * rows, rows)
        return pltpu.make_async_copy(w_hbm.at[at], wbuf.at[at], w_sem.at[c])

    seed_copy = pltpu.make_async_copy(seed_hbm, gbuf, seed_sem)
    acts_copy = pltpu.make_async_copy(acts_hbm, abuf, a_sem)

    @pl.when(s == sections - 1)
    def _():
        seed_copy.start()

    acts_copy.start()

    @pl.when(s > 0)
    def _():
        for c in range(CHUNKS):
            w_copy(c).start()

    acts_copy.wait()
    dabuf[...] = fdot(down_ref[...], abuf[...], NT).astype(jnp.bfloat16)

    @pl.when(s == sections - 1)
    def _():
        seed_copy.wait()

    @pl.when(s > 0)
    def _():
        for c in range(CHUNKS):
            w_copy(c).wait()

    pl.semaphore_wait(barrier, sections - 1 + replicas - 1)

    def hop(m, c):
        at = pl.ds(pl.multiple_of(c * rows, rows), rows)
        return pltpu.make_async_remote_copy(
            src_ref=obuf.at[m, at],
            dst_ref=gbuf.at[m, at],
            send_sem=send_sem.at[m, c],
            recv_sem=recv_sem.at[m, c],
            device_id=((s + sections - 1) % sections, d),
            device_id_type=MESH,
        )

    def slot(m, carry):
        @pl.when(s < sections - 1)
        def _():
            for c in range(CHUNKS):
                hop(m, c).wait_recv()

        up_grad = fdot(up_ref[...], gbuf[m]).astype(jnp.bfloat16)
        ugbuf[...] = up_grad

        @pl.when(s > 0)
        def _():
            def chunk(c, carry):
                at = pl.ds(pl.multiple_of(c * rows, rows), rows)
                got = fdot(wbuf[at, :], gbuf[m]) + fdot(downt_ref[at, :], ugbuf[...])
                obuf[m, at, :] = got.astype(jnp.bfloat16)
                hop(m, c).start()
                return carry

            lax.fori_loop(0, CHUNKS, chunk, 0)

        inputs = abuf[pl.ds(pl.multiple_of(m * tokens, tokens), tokens), :]
        down_act = dabuf[:, pl.ds(pl.multiple_of(m * tokens, tokens), tokens)]
        down_term = fdot(ugbuf[...], inputs)
        up_term = fdot(down_act, gbuf[m], NT)
        tbuf[m, :rank, :] = down_term
        tbuf[m, rank:, :] = up_term
        square = jnp.sum(down_term * down_term + up_term * up_term, axis=0, keepdims=True)
        square = jnp.sum(square, axis=1, keepdims=True)
        sqbuf[pl.ds(m, 1), :] = jnp.broadcast_to(square, (1, LANES))
        return carry

    sqbuf[...] = jnp.zeros_like(sqbuf)
    redsend[:, features:] = jnp.zeros_like(redsend[:, features:])
    lax.fori_loop(0, slots, slot, 0)

    def sq_hop(k):
        return pltpu.make_async_remote_copy(
            src_ref=sqbuf, dst_ref=sqall.at[s],
            send_sem=sqs_sem.at[k], recv_sem=sqr_sem.at[k],
            device_id=((s + k) % sections, d), device_id_type=MESH,
        )

    for k in range(1, sections):
        sq_hop(k).start()
    sqall[s] = sqbuf[...]
    for k in range(1, sections):
        sq_hop(k).wait_recv()
    norm = jnp.sqrt(jnp.sum(sqall[...], axis=0))
    norm_ref[...] = norm
    factor = clip_scale / (norm + 0.01)
    total = factor[0:1, 0:1] * tbuf[0]
    for m in range(1, slots):
        total = total + factor[m : m + 1, 0:1] * tbuf[m]
    redsend[:, :features] = total.astype(jnp.bfloat16)

    def window_of(t):
        return pl.ds(pl.multiple_of(span * t // LANES * LANES, LANES), window)

    def red_hop(k):
        t = (d + k) % replicas
        return pltpu.make_async_remote_copy(
            src_ref=redsend.at[:, window_of(t)], dst_ref=redin.at[d],
            send_sem=rs_sem.at[k], recv_sem=rr_sem.at[k],
            device_id=(s, t), device_id_type=MESH,
        )

    for k in range(1, replicas):
        red_hop(k).start()
    redin[d] = redsend[:, window_of(d)]
    for k in range(1, replicas):
        red_hop(k).wait_recv()
    red_ref[...] = jnp.sum(redin[...].astype(jnp.float32), axis=0)

    @pl.when(s > 0)
    def _():
        def drain(m, carry):
            for c in range(CHUNKS):
                hop(m, c).wait_send()
            return carry

        lax.fori_loop(0, slots, drain, 0)

    for k in range(1, sections):
        sq_hop(k).wait_send()
    for k in range(1, replicas):
        red_hop(k).wait_send()


def on_device(acts, cotangent, frozen, down_adapter, up_adapter, example_ids, lengths):
    sections = lax.axis_size("section")
    replicas = lax.axis_size("dp")
    layer_inputs = acts[0]
    slots = example_ids.shape[1]
    features = layer_inputs.shape[1]
    tokens = layer_inputs.shape[0] // slots
    rank = down_adapter.shape[1]
    choose = (example_ids[0][:, None] == jnp.arange(slots, dtype=jnp.int32)[None, :]).astype(jnp.int32)
    slot_length = jnp.sum(choose * lengths[0][None, :], axis=1)
    live = (jnp.arange(tokens, dtype=jnp.int32)[None, :] < slot_length[:, None]).astype(jnp.bfloat16)
    seeded = cotangent.reshape(slots, tokens, features) * live[:, :, None]
    seeded = jnp.swapaxes(seeded, 1, 2)
    clip_scale = math.sqrt(2.0 * rank * features) / math.sqrt(replicas * slots)
    weight = lax.all_gather(frozen[0], "dp", axis=0, tiled=True)
    span = features // replicas
    window = -(-(span + LANES - 1) // LANES) * LANES
    vmem = pl.BlockSpec(memory_space=pltpu.VMEM)
    hbm = pl.BlockSpec(memory_space=pl.ANY)
    dma = pltpu.SemaphoreType.DMA
    bf16, f32 = jnp.bfloat16, jnp.float32
    reduced, norms = pl.pallas_call(
        functools.partial(kernel, sections, replicas, clip_scale),
        out_shape=(
            jax.ShapeDtypeStruct((2 * rank, window), f32),
            jax.ShapeDtypeStruct((8, LANES), f32),
        ),
        in_specs=[hbm, hbm, hbm, vmem, vmem, vmem],
        out_specs=(vmem, vmem),
        scratch_shapes=[
            pltpu.VMEM((features, features), bf16),
            pltpu.VMEM((slots, features, tokens), bf16),
            pltpu.VMEM((slots, features, tokens), bf16),
            pltpu.VMEM((slots * tokens, features), bf16),
            pltpu.VMEM((rank, tokens), bf16),
            pltpu.VMEM((rank, slots * tokens), bf16),
            pltpu.VMEM((slots, 2 * rank, features), f32),
            pltpu.VMEM((8, LANES), f32),
            pltpu.VMEM((sections, 8, LANES), f32),
            pltpu.VMEM((2 * rank, features + LANES), bf16),
            pltpu.VMEM((replicas, 2 * rank, window), bf16),
            dma((CHUNKS,)), dma, dma,
            dma((slots, CHUNKS)), dma((slots, CHUNKS)),
            dma((sections,)), dma((sections,)),
            dma((replicas,)), dma((replicas,)),
        ],
        compiler_params=pltpu.CompilerParams(
            collective_id=0, has_side_effects=True, vmem_limit_bytes=60 * 1024 * 1024
        ),
    )(weight, seeded, layer_inputs, up_adapter[0], down_adapter[0], down_adapter[0].T)
    shift = span * lax.axis_index("dp") % LANES
    mine = lax.dynamic_slice_in_dim(reduced, shift, span, axis=1)
    slot_norms = norms[:slots, 0]
    example_norms = jnp.sum(choose.astype(f32) * slot_norms[:, None], axis=0)
    return (mine[None, :rank], mine[None, rank:], example_norms[None])


def solution(mesh):
    in_specs = (
        P("section", "dp", None),
        P("dp", None),
        P("section", "dp", None),
        P("section", None, None),
        P("section", None, None),
        P("dp", None),
        P("dp", None),
    )
    out_specs = (P("section", None, "dp"), P("section", None, "dp"), P("dp", None))
    return jax.shard_map(
        on_device, mesh=mesh, in_specs=in_specs, out_specs=out_specs, check_vma=False
    )
```

time: 539 us -> 312 us (0.58)
  waiting for transfers between devices: 357 us -> 151 us
  Pallas kernels: 0 us -> 131 us
  matrix products: 70.1 us -> 0 us
  starting transfers between devices: 30.6 us -> 0.04 us
  other arithmetic: 34.6 us -> 4.92 us
  local copies, waits for them, and re-layouts: 25 us -> 9.58 us
  blocking collectives: 6.18 us -> 0 us
    ppermute x11 -> x0, waiting for transfers between devices: 189 us -> none  [from_behind(): lax.ppermute(value, axis, [(source, source + steps) for source in range(f...]
    pallas_call x0 -> x1, Pallas kernels: none -> 131 us  [on_device(): pl.pallas_call(functools.partial(kernel, sections, replicas, clip_scale),...]
    dot_general x10 -> x0, matrix products: 70.1 us -> none  [the longest x4 51.6 us: backstep(): in_grad = jnp.dot(out_grad, weight.T, preferred_element_type=jnp.float32)]
    dynamic_update_slice x11 -> x0, other arithmetic: 28.6 us -> none  [tick_step(): lax.dynamic_update_index_in_dim(stored_grads, kept, held_index, 0)]
    ppermute x11 -> x0, starting transfers between devices: 25.5 us -> none  [from_behind(): lax.ppermute(value, axis, [(source, source + steps) for source in range(f...]
    dynamic_slice x11 -> x0, local copies, waits for them, and re-layouts: 13.6 us -> none  [tick_step(): lax.dynamic_index_in_dim(stored_grads, held_index, 0, keepdims=False)]
    all_to_all x1 -> x0, waiting for transfers between devices: 9.8 us -> none  [sent_and_summed(): lax.all_to_all(pieces, axis, split_axis=0, concat_axis=0, tiled=True)]
    another operation x8 -> x0, local copies, waits for them, and re-layouts: 7.19 us -> none
  transfers between devices with their start and end apart: 13 -> 1, of which waited for: 13 -> 1; matrix products, arithmetic and copies ran while one was open for 1% -> 4% of each run, Pallas kernels for 0% -> 0%
where the time goes in v1:
time: 312 us; the launch traced here: 311 us
  waiting for transfers between devices  151 us (48%)
  Pallas kernels  131 us (42%)
  between operations  14.1 us (5%)
  local copies, waits for them, and re-layouts  9.58 us (3%)
  other arithmetic  4.92 us (2%)
    all_gather x1, waiting for transfers between devices, on_device(): weight = lax.all_gather(frozen[0], 'dp', axis=0, tiled=True)  150 us
    pallas_call x1, Pallas kernels, on_device(): pl.pallas_call(functools.partial(kernel, sections, replicas, clip_scale),...  131 us
  transfers between devices with their start and end apart: 1, of which 1 were waited for; matrix products, arithmetic and copies ran while one was open for 4% of the time, Pallas kernels for 0%

profile of v1, /device:TPU:1, one launch (start us, length us, event | category | flops | bytes accessed | tf_op | source)
XLA Modules:
  0.0 311.2 jit_solution(14916831017657241322)
XLA Ops:
  7.2 0.0 all-gather.3.cloned.1.call-start
  7.2 0.7 all-gather.3.cloned.1.call-update
  7.9 0.0 copy-start
  7.9 0.0 copy-start.1
  7.9 0.0 copy-start.2
  7.9 6.0 %copy.15 = bf16[4,128,3584]{1,2,0:T(8,128)(2,1)} copy(bf16[4,128,3584]{2,1,0:T(8,128)(2,1)} %bitcast.19) | data formatting | bytes 7340032 | tf_op jit(solution)/shard_map/reshape | solution.py:186
  14.0 0.0 copy-done
  14.0 1.3 copy.16
  15.3 0.0 copy-done.1
  15.3 0.0 copy-done.2
  15.3 0.2 select_reduce_fusion
  15.5 0.1 fusion
  15.5 4.1 %multiply_bitcast_fusion.seed_hbm = bf16[4,3584,128]{2,1,0:T(8,128)(2,1)} fusion(bf16[4,128,3584]{1,2,0:T(8,128)(2,1)} %copy.15, bf16[4,128]{1,0:T(4,128)(2,1)S(1)} %fusion), kind=kLoop, calls=%fused_computation | loop fusion | flops 1835008 | bytes 7341056 | tf_op jit(solution)/shard_map/transpose | solution.py:187
  19.6 150.5 %all-gather.3.cloned.1.call-done = bf16[1,3584,3584]{2,1,0:T(8,128)(2,1)} async-done(((bf16[1,224,3584]{2,1,0:T(8,128)(2,1)}), bf16[1,3584,3584]{2,1,0:T(8,128)(2,1)}) %all-gather.3.cloned.1.call-update) | async-done | bytes 25690128 | tf_op jit(solution)/shard_map/all_gather | solution.py:189
  170.1 131.4 %shard_map.94 = (f32[32,384]{1,0:T(8,128)}, f32[8,128]{1,0:T(8,128)}) custom-call(bf16[3584,3584]{1,0:T(8,128)(2,1)} %bitcast.17, bf16[4,3584,128]{2,1,0:T(8,128)(2,1)} %multiply_bitcast_fusion.seed_hbm, bf16[512,3584]{1,0:T(8,128)(2,1)} %bitcast.18, bf16[16,3584]{1,0:T(8,128)(2,1)} %bitcast.22, bf16[16,3584]{1,0:T(8,128)(2,1)} %bitcast.21, ...), custom_call_target="tpu_custom_call" | custom-call | tf_op jit(solution)/shard_map/pallas_call | solution.py:196
  301.5 0.8 slice_reduce_fusion
  302.3 0.6 multiply_reduce_fusion
  302.9 1.4 dynamic-slice_bitcast_fusion
Async XLA Ops:
  7.2 162.9 %all-gather.3.cloned.1.call-start = ((), (), s32[]{:S(2)}) async-start(), calls=%async_computation | async-start | bytes 27295744 | tf_op jit(solution)/shard_map/all_gather | solution.py:189
  7.9 6.1 %copy-start = (bf16[1,16,3584]{2,1,0:T(8,128)(2,1)S(1)}, bf16[1,16,3584]{2,1,0:T(8,128)(2,1)}, u32[]{:S(2)}) copy-start(bf16[1,16,3584]{2,1,0:T(8,128)(2,1)} %param.10) | copy-start | bytes 344068
  7.9 7.4 %copy-start.1 = (s32[1,4]{1,0:T(1,128)S(1)}, s32[1,4]{1,0:T(1,128)}, u32[]{:S(2)}) copy-start(s32[1,4]{1,0:T(1,128)} %param.13) | copy-start | bytes 52
  7.9 7.3 %copy-start.2 = (s32[1,4]{1,0:T(1,128)S(1)}, s32[1,4]{1,0:T(1,128)}, u32[]{:S(2)}) copy-start(s32[1,4]{1,0:T(1,128)} %param.12) | copy-start | bytes 52
Sparse Core Ops, SparseCore 0:
  10.1 159.9 all-gather.2

commit v2 on v1

v2 whole, which is shorter than its diff:
```python
import functools
import math

import jax
import jax.numpy as jnp
from jax import lax
from jax.experimental import pallas as pl
from jax.experimental.pallas import tpu as pltpu
from jax.sharding import PartitionSpec as P

MESH = pl.DeviceIdType.MESH
NT = (((1,), (1,)), ((), ()))
LANES = 128
SIDE = 4
SUBS = 4
QUADS = 4


def fdot(a, b, dims=None):
    if dims is None:
        return jnp.dot(a, b, preferred_element_type=jnp.float32)
    return lax.dot_general(a, b, dims, preferred_element_type=jnp.float32)


def kernel(
    sections, replicas, slots, clip_scale,
    frozen_hbm, cot_hbm, acts_hbm, up_ref, down_ref, live_ref,
    red_ref, norm_ref,
    wbuf, gbuf, obuf, abuf, cbuf, upb, downb, dtb, ugb, dab, tbuf, sqbuf, sqall, redsend, redin,
    local_sem, swap_send, swap_recv, ws, wr, es, er, ys, yr, fs, fr, sqs, sqr, rs, rr,
):
    s = lax.axis_index("section")
    d = lax.axis_index("dp")
    y, c = s // 2, s % 2
    top = y == sections // 2 - 1
    half = wbuf.shape[2]
    features = wbuf.shape[3]
    width = gbuf.shape[4]
    tokens = width // slots
    rank = up_ref.shape[0]
    span = features // replicas
    window = redin.shape[2]
    cols = features // SUBS
    group = replicas // QUADS
    partner = s + 1 - 2 * c
    below = (s + sections - 2) % sections
    mine = 1 - c

    z, x = d // SIDE, d % SIDE
    q = (x + 1) % SIDE
    p = (1 - c) * (SIDE * z + (z + x) % SIDE) + c * (SIDE * q + (z + q + 3) % SIDE)

    def device_at(pos):
        pos = (pos + 2 * replicas) % replicas
        hi, lo = pos // SIDE, pos % SIDE
        first = SIDE * hi + (lo + SIDE - hi) % SIDE
        second = SIDE * ((lo + 1 + SIDE - hi) % SIDE) + (hi + 3) % SIDE
        return (1 - c) * first + c * second

    def remote(src, dst, send, recv, device):
        return pltpu.make_async_remote_copy(
            src_ref=src, dst_ref=dst, send_sem=send, recv_sem=recv,
            device_id=device, device_id_type=MESH,
        )

    barrier = pltpu.get_barrier_semaphore()
    for k in range(1, sections):
        pl.semaphore_signal(barrier, inc=1, device_id=((s + k) % sections, d), device_id_type=MESH)
    for k in range(1, replicas):
        pl.semaphore_signal(barrier, inc=1, device_id=(s, (d + k) % replicas), device_id_type=MESH)

    def half_rows(h):
        return frozen_hbm.at[pl.ds(pl.multiple_of(h * half, 16), half)]

    own_copy = pltpu.make_async_copy(half_rows(c), wbuf.at[mine, d], local_sem.at[0])
    acts_copy = pltpu.make_async_copy(acts_hbm, abuf, local_sem.at[1])
    cot_copy = pltpu.make_async_copy(cot_hbm, cbuf, local_sem.at[2])
    own_copy.start()
    acts_copy.start()

    @pl.when(top)
    def _():
        cot_copy.start()

    upb[mine] = up_ref[...]
    downb[mine] = down_ref[...]
    sqbuf[...] = jnp.zeros_like(sqbuf)
    redsend[:, features:] = jnp.zeros_like(redsend[:, features:])
    pl.semaphore_wait(barrier, sections - 1 + replicas - 1)

    def swaps(j):
        to = (partner, d)
        return (
            remote(half_rows(1 - c), wbuf.at[j, d], swap_send.at[0], swap_recv.at[0], to),
            remote(up_ref, upb.at[j], swap_send.at[1], swap_recv.at[1], to),
            remote(down_ref, downb.at[j], swap_send.at[2], swap_recv.at[2], to),
        )

    for copy in swaps(mine):
        copy.start()
    own_copy.wait()
    for copy in swaps(c):
        copy.wait_recv()

    def ring(j, way, k, sub, origin):
        at = wbuf.at[j, device_at(origin), :, pl.ds(pl.multiple_of(sub * cols, LANES), cols)]
        to = (s, device_at(p + 1 - 2 * way))
        return remote(at, at, ws.at[j, way, k - 1, sub], wr.at[j, way, k - 1, sub], to)

    def sending(j, way, k, sub):
        return ring(j, way, k, sub, p - (1 - 2 * way) * (k - 1))

    def arriving(j, way, k, sub):
        return ring(j, way, k, sub, p - (1 - 2 * way) * k)

    last = replicas // 2

    def begin(j):
        for sub in range(SUBS):
            for way in range(2):
                sending(j, way, 1, sub).start()

    def serve(j, k, sub):
        for way in range(2):
            ours = (sub < SUBS // 2) if way == 0 else (sub >= SUBS // 2)

            @pl.when((k < last) | ours)
            def _(way=way):
                arriving(j, way, k, sub).wait_recv()

            @pl.when((k < last - 1) | ((k == last - 1) & ours))
            def _(way=way):
                sending(j, way, k + 1, sub).start()

    def waves(j, first, count, work=None):
        def wave(w, carry):
            serve(j, first + w // SUBS, w % SUBS)
            if work is not None:
                work(w)
            return carry

        lax.fori_loop(0, count, wave, 0)

    def lanes(m):
        return pl.ds(pl.multiple_of(m * tokens, LANES), tokens)

    def seed(w):
        @pl.when(top)
        def _():
            m, part = w // QUADS, w % QUADS
            wide = features // QUADS
            block = cbuf[
                pl.ds(pl.multiple_of(m * tokens, tokens), tokens),
                pl.ds(pl.multiple_of(part * wide, LANES), wide),
            ]
            turned = block.astype(jnp.float32).T * live_ref[0:1, lanes(m)]
            gbuf[0, pl.ds(part * group, group), :, :, lanes(m)] = turned.astype(jnp.bfloat16).reshape(
                group, 2, half, tokens
            )

    begin(0)

    @pl.when(top)
    def _():
        cot_copy.wait()

    waves(0, 1, 16, seed)
    acts_copy.wait()
    dab[...] = fdot(down_ref[...], abuf[...], NT).astype(jnp.bfloat16)
    for j in range(2):
        turned = downb[j].astype(jnp.float32).T
        dtb[j] = turned.astype(jnp.bfloat16).reshape(replicas, 2, half, rank)

    def whole(j):
        return gbuf[j].reshape(features, width)

    def part_of(j, m):
        return gbuf[j, :, :, :, lanes(m)].reshape(features, tokens)

    @pl.when(top)
    def _():
        ugb[0] = fdot(upb[0], whole(0)).astype(jnp.bfloat16)

    waves(0, 5, 12)
    begin(1)
    waves(0, 8, 4)

    def top_product(j, o):
        got = fdot(wbuf[j, o], whole(j)) + fdot(dtb[j, o, c], ugb[j])
        return got.astype(jnp.bfloat16)

    def across(o):
        at = gbuf.at[1, o, c]
        return remote(at, at, es.at[o], er.at[o], (partner, d))

    def across_in(o):
        at = gbuf.at[1, o, 1 - c]
        return remote(at, at, es.at[o], er.at[o], (partner, d))

    def down_hop(o):
        return remote(obuf.at[o], gbuf.at[0, o, c], ys.at[o], yr.at[o], (below, d))

    def relay(o):
        at = gbuf.at[0, o, c]
        return remote(at, at, fs.at[o], fr.at[o], (partner, d))

    def relay_in(o):
        at = gbuf.at[0, o, 1 - c]
        return remote(at, at, fs.at[o], fr.at[o], (partner, d))

    def block_at(r):
        return device_at(p - (r % 2) * ((r + 1) // 2) + (1 - r % 2) * (r // 2))

    def upper(w):
        @pl.when(top)
        def _():
            def one(i, carry):
                o = 2 * w + i
                gbuf[1, o, c] = top_product(0, o)
                across(o).start()
                return carry

            lax.fori_loop(0, 2, one, 0)

    def lower(r):
        o = block_at(r)
        obuf[o] = top_product(1, o)
        down_hop(o).start()

    def hand_on(r):
        o = block_at(r)
        down_hop_in(o).wait_recv()
        relay(o).start()

    def down_hop_in(o):
        return remote(obuf.at[o], gbuf.at[0, o, c], ys.at[o], yr.at[o], (below, d))

    waves(1, 1, 8, upper)

    @pl.when(top)
    def _():
        def one(o, carry):
            across_in(o).wait_recv()
            return carry

        lax.fori_loop(0, replicas, one, 0)
        ugb[1] = fdot(upb[1], whole(1)).astype(jnp.bfloat16)

    second = y == sections // 2 - 2

    def middle(w):
        @pl.when(top & ((w < 4) | (w % 2 == 0)))
        def _():
            lower(jnp.where(w < 4, w, 2 + w // 2))

        @pl.when(second & (w >= 4) & (w % 2 == 1))
        def _():
            hand_on((w - 4) // 2)

    waves(1, 3, 20, middle)

    def final(w):
        @pl.when(top)
        def _():
            lower(12 + w)

    def final_three(w):
        @pl.when(top & (w < 3))
        def _():
            lower(12 + w)

    waves(1, 8, 4, final_three)

    @pl.when(top)
    def _():
        lower(15)

    @pl.when(second)
    def _():
        def one(r, carry):
            hand_on(r)
            return carry

        lax.fori_loop(8, replicas, one, 0)

        def two(o, carry):
            relay_in(o).wait_recv()
            return carry

        lax.fori_loop(0, replicas, two, 0)

    def terms(m):
        inputs = abuf[pl.ds(pl.multiple_of(m * tokens, tokens), tokens), :]
        down_term = fdot(ugb[mine, :, lanes(m)], inputs)
        up_term = fdot(dab[:, lanes(m)], part_of(mine, m), NT)
        tbuf[m, :rank, :] = down_term
        tbuf[m, rank:, :] = up_term
        square = jnp.sum(down_term * down_term + up_term * up_term, axis=0, keepdims=True)
        square = jnp.sum(square, axis=1, keepdims=True)
        sqbuf[pl.ds(m, 1), :] = jnp.broadcast_to(square, (1, LANES))

    def quad(ref, j, m, part, side):
        return ref.at[j, pl.ds(part * group, group), side, :, lanes(m)]

    def quad_product(j, m, part):
        blocks = pl.ds(part * group, group)
        weight = wbuf[j, blocks].reshape(group * half, features)
        adapter = dtb[j, blocks, c].reshape(group * half, rank)
        got = fdot(weight, part_of(j, m)) + fdot(adapter, ugb[j, :, lanes(m)])
        return got.astype(jnp.bfloat16).reshape(group, half, tokens)

    def quad_across(m, part, side):
        at = quad(gbuf, 1, m, part, side)
        return remote(at, at, es.at[m * QUADS + part], er.at[m * QUADS + part], (partner, d))

    def quad_down(m, part):
        src = obuf.at[pl.ds(part * group, group), :, lanes(m)]
        at = m * QUADS + part
        return remote(src, quad(gbuf, 0, m, part, c), ys.at[at], yr.at[at], (below, d))

    def quad_relay(m, part, side):
        at = quad(gbuf, 0, m, part, side)
        return remote(at, at, fs.at[m * QUADS + part], fr.at[m * QUADS + part], (partner, d))

    def each_quad(work):
        def one(part, carry):
            work(part)
            return carry

        lax.fori_loop(0, QUADS, one, 0)

    def slot(m, carry):
        @pl.when(y < sections // 2 - 2)
        def _():
            def pass_on(part):
                quad_down(m, part).wait_recv()
                quad_relay(m, part, c).start()

            each_quad(pass_on)
            each_quad(lambda part: quad_relay(m, part, 1 - c).wait_recv())

        ugb[0, :, lanes(m)] = fdot(upb[0], part_of(0, m)).astype(jnp.bfloat16)

        def odd(part):
            gbuf[1, pl.ds(part * group, group), c, :, lanes(m)] = quad_product(0, m, part)
            quad_across(m, part, c).start()

        each_quad(odd)

        @pl.when(c == 1)
        def _():
            terms(m)

        each_quad(lambda part: quad_across(m, part, 1 - c).wait_recv())
        ugb[1, :, lanes(m)] = fdot(upb[1], part_of(1, m)).astype(jnp.bfloat16)

        @pl.when(y > 0)
        def _():
            def even(part):
                obuf[pl.ds(part * group, group), :, lanes(m)] = quad_product(1, m, part)
                quad_down(m, part).start()

            each_quad(even)

        @pl.when(c == 0)
        def _():
            terms(m)

        return carry

    @pl.when(y < sections // 2 - 1)
    def _():
        lax.fori_loop(0, slots, slot, 0)

    @pl.when(top)
    def _():
        def one(m, carry):
            terms(m)
            return carry

        lax.fori_loop(0, slots, one, 0)

    def sq_hop(k):
        return remote(sqbuf, sqall.at[s], sqs.at[k], sqr.at[k], ((s + k) % sections, d))

    for k in range(1, sections):
        sq_hop(k).start()
    sqall[s] = sqbuf[...]
    for k in range(1, sections):
        sq_hop(k).wait_recv()
    norm = jnp.sqrt(jnp.sum(sqall[...], axis=0))
    norm_ref[...] = norm
    factor = clip_scale / (norm + 0.01)
    total = factor[0:1, 0:1] * tbuf[0]
    for m in range(1, slots):
        total = total + factor[m : m + 1, 0:1] * tbuf[m]
    redsend[:, :features] = total.astype(jnp.bfloat16)

    def window_of(t):
        return pl.ds(pl.multiple_of(span * t // LANES * LANES, LANES), window)

    def red_hop(k):
        t = (d + k) % replicas
        return remote(redsend.at[:, window_of(t)], redin.at[d], rs.at[k], rr.at[k], (s, t))

    for k in range(1, replicas):
        red_hop(k).start()
    redin[d] = redsend[:, window_of(d)]
    for k in range(1, replicas):
        red_hop(k).wait_recv()
    red_ref[...] = jnp.sum(redin[...].astype(jnp.float32), axis=0)

    for copy in swaps(mine):
        copy.wait_send()
    for j in range(2):

        def one(w, carry):
            k, sub = 1 + w // SUBS, w % SUBS
            for way in range(2):
                ours = (sub < SUBS // 2) if way == 0 else (sub >= SUBS // 2)

                @pl.when((k < last) | ours)
                def _(way=way):
                    sending(j, way, k, sub).wait_send()

            return carry

        lax.fori_loop(0, last * SUBS, one, 0)

    @pl.when(top)
    def _():
        def one(o, carry):
            across(o).wait_send()
            down_hop(o).wait_send()
            return carry

        lax.fori_loop(0, replicas, one, 0)

    @pl.when(second)
    def _():
        def one(o, carry):
            relay(o).wait_send()
            return carry

        lax.fori_loop(0, replicas, one, 0)

    @pl.when(y < sections // 2 - 1)
    def _():
        def one(w, carry):
            m, part = w // QUADS, w % QUADS
            quad_across(m, part, c).wait_send()

            @pl.when(y > 0)
            def _():
                quad_down(m, part).wait_send()

            @pl.when(y < sections // 2 - 2)
            def _():
                quad_relay(m, part, c).wait_send()

            return carry

        lax.fori_loop(0, slots * QUADS, one, 0)

    for k in range(1, sections):
        sq_hop(k).wait_send()
    for k in range(1, replicas):
        red_hop(k).wait_send()


def on_device(acts, cotangent, frozen, down_adapter, up_adapter, example_ids, lengths):
    sections = lax.axis_size("section")
    replicas = lax.axis_size("dp")
    layer_inputs = acts[0]
    slots = example_ids.shape[1]
    width, features = layer_inputs.shape
    tokens = width // slots
    rank = down_adapter.shape[1]
    choose = (example_ids[0][:, None] == jnp.arange(slots, dtype=jnp.int32)[None, :]).astype(jnp.int32)
    slot_length = jnp.sum(choose * lengths[0][None, :], axis=1)
    live = (jnp.arange(tokens, dtype=jnp.int32)[None, :] < slot_length[:, None]).astype(jnp.float32)
    live = jnp.broadcast_to(live.reshape(1, width), (8, width))
    clip_scale = math.sqrt(2.0 * rank * features) / math.sqrt(replicas * slots)
    span = features // replicas
    half = span // 2
    window = -(-(span + LANES - 1) // LANES) * LANES
    vmem = pl.BlockSpec(memory_space=pltpu.VMEM)
    hbm = pl.BlockSpec(memory_space=pl.ANY)
    dma = pltpu.SemaphoreType.DMA
    bf16, f32 = jnp.bfloat16, jnp.float32
    reduced, norms = pl.pallas_call(
        functools.partial(kernel, sections, replicas, slots, clip_scale),
        out_shape=(
            jax.ShapeDtypeStruct((2 * rank, window), f32),
            jax.ShapeDtypeStruct((8, LANES), f32),
        ),
        in_specs=[hbm, hbm, hbm, vmem, vmem, vmem],
        out_specs=(vmem, vmem),
        scratch_shapes=[
            pltpu.VMEM((2, replicas, half, features), bf16),
            pltpu.VMEM((2, replicas, 2, half, width), bf16),
            pltpu.VMEM((replicas, half, width), bf16),
            pltpu.VMEM((width, features), bf16),
            pltpu.VMEM((width, features), bf16),
            pltpu.VMEM((2, rank, features), bf16),
            pltpu.VMEM((2, rank, features), bf16),
            pltpu.VMEM((2, replicas, 2, half, rank), bf16),
            pltpu.VMEM((2, rank, width), bf16),
            pltpu.VMEM((rank, width), bf16),
            pltpu.VMEM((slots, 2 * rank, features), f32),
            pltpu.VMEM((8, LANES), f32),
            pltpu.VMEM((sections, 8, LANES), f32),
            pltpu.VMEM((2 * rank, features + LANES), bf16),
            pltpu.VMEM((replicas, 2 * rank, window), bf16),
            dma((3,)), dma((3,)), dma((3,)),
            dma((2, 2, replicas // 2, SUBS)), dma((2, 2, replicas // 2, SUBS)),
            dma((replicas,)), dma((replicas,)),
            dma((replicas,)), dma((replicas,)),
            dma((replicas,)), dma((replicas,)),
            dma((sections,)), dma((sections,)),
            dma((replicas,)), dma((replicas,)),
        ],
        compiler_params=pltpu.CompilerParams(
            collective_id=0, has_side_effects=True, vmem_limit_bytes=62 * 1024 * 1024
        ),
    )(frozen[0], cotangent, layer_inputs, up_adapter[0], down_adapter[0], live)
    shift = span * lax.axis_index("dp") % LANES
    mine = lax.dynamic_slice_in_dim(reduced, shift, span, axis=1)
    slot_norms = norms[:slots, 0]
    example_norms = jnp.sum(choose.astype(f32) * slot_norms[:, None], axis=0)
    return (mine[None, :rank], mine[None, rank:], example_norms[None])


def solution(mesh):
    in_specs = (
        P("section", "dp", None),
        P("dp", None),
        P("section", "dp", None),
        P("section", None, None),
        P("section", None, None),
        P("dp", None),
        P("dp", None),
    )
    out_specs = (P("section", None, "dp"), P("section", None, "dp"), P("dp", None))
    return jax.shard_map(
        on_device, mesh=mesh, in_specs=in_specs, out_specs=out_specs, check_vma=False
    )
```

time: 312 us -> 256 us (0.82)
  waiting for transfers between devices: 151 us -> 0 us
  Pallas kernels: 131 us -> 250 us
  between operations: 14.1 us -> 0.66 us
  local copies, waits for them, and re-layouts: 9.58 us -> 2.87 us
  other arithmetic: 4.92 us -> 1.53 us
    all_gather x1 -> x0, waiting for transfers between devices: 150 us -> none  [on_device(): weight = lax.all_gather(frozen[0], 'dp', axis=0, tiled=True)]
    pallas_call x1, Pallas kernels: 131 us -> 250 us  [on_device(): pl.pallas_call(functools.partial(kernel, sections, replicas, slots, clip_...]
    reshape x1 -> x0, local copies, waits for them, and re-layouts: 6.03 us -> none  [on_device(): seeded = cotangent.reshape(slots, tokens, features) * live[:, :, None]]
    transpose x1 -> x0, other arithmetic: 4.06 us -> none  [on_device(): seeded = jnp.swapaxes(seeded, 1, 2)]
  transfers between devices with their start and end apart: 1 -> 0, of which waited for: 1 -> 0; matrix products, arithmetic and copies ran while one was open for 4% -> 0% of each run, Pallas kernels for 0% -> 0%
where the time goes in v2:
time: 256 us; the launch traced here: 255 us
  Pallas kernels  250 us (98%)
  local copies, waits for them, and re-layouts  2.87 us (1%)
    pallas_call x1, Pallas kernels, on_device(): pl.pallas_call(functools.partial(kernel, sections, replicas, slots, clip_...  250 us

profile of v2, /device:TPU:1, one launch (start us, length us, event | category | flops | bytes accessed | tf_op | source)
XLA Modules:
  0.0 254.7 jit_solution(3111746912017927147)
XLA Ops:
  0.6 0.9 select_reduce_fusion
  1.5 0.1 convert_bitcast_fusion
  1.6 0.6 broadcast_in_dim.8.live_ref
  2.2 0.0 copy-start
  2.2 249.7 %shard_map.94 = (f32[32,384]{1,0:T(8,128)}, f32[8,128]{1,0:T(8,128)}) custom-call(bf16[224,3584]{1,0:T(8,128)(2,1)} %bitcast.14, bf16[512,3584]{1,0:T(8,128)(2,1)} %cot_hbm.1, bf16[512,3584]{1,0:T(8,128)(2,1)} %bitcast.13, bf16[16,3584]{1,0:T(8,128)(2,1)} %bitcast.15, bf16[16,3584]{1,0:T(8,128)(2,1)} %bitcast.16, f32[8,512]{1,0:T(8,128)} %broadcast_in_dim.8.live_ref), custom_call_target="tpu_custom_call" | custom-call | tf_op jit(solution)/shard_map/pallas_call | solution.py:491
  251.9 1.5 dynamic-slice_bitcast_fusion
  253.3 0.8 slice_reduce_fusion
  254.1 0.0 copy-done
  254.1 0.6 multiply_reduce_fusion
Async XLA Ops:
  2.2 251.9 %copy-start = (s32[1,4]{1,0:T(1,128)S(1)}, s32[1,4]{1,0:T(1,128)}, u32[]{:S(2)}) copy-start(s32[1,4]{1,0:T(1,128)} %param.12) | copy-start | bytes 52

commit v3 on v2

--- a/solution.py
+++ b/solution.py
@@ -24,10 +24,12 @@
 
 def kernel(
     sections, replicas, slots, clip_scale,
-    frozen_hbm, cot_hbm, acts_hbm, up_ref, down_ref, live_ref,
-    red_ref, norm_ref,
+    frozen_hbm, cot_hbm, acts_hbm, up_ref, down_ref, ids_ref, lengths_ref,
+    out_ref,
     wbuf, gbuf, obuf, abuf, cbuf, upb, downb, dtb, ugb, dab, tbuf, sqbuf, sqall, redsend, redin,
+    live,
     local_sem, swap_send, swap_recv, ws, wr, es, er, ys, yr, fs, fr, sqs, sqr, rs, rr,
+    y2s, y2r, f2s, f2r,
 ):
     s = lax.axis_index("section")
     d = lax.axis_index("dp")
@@ -57,6 +59,15 @@
         second = SIDE * ((lo + 1 + SIDE - hi) % SIDE) + (hi + 3) % SIDE
         return (1 - c) * first + c * second
 
+    p2 = c * (SIDE * z + (z + x) % SIDE) + (1 - c) * (SIDE * q + (z + q + 3) % SIDE)
+
+    def other_device_at(pos):
+        pos = (pos + 2 * replicas) % replicas
+        hi, lo = pos // SIDE, pos % SIDE
+        first = SIDE * hi + (lo + SIDE - hi) % SIDE
+        second = SIDE * ((lo + 1 + SIDE - hi) % SIDE) + (hi + 3) % SIDE
+        return c * first + (1 - c) * second
+
     def remote(src, dst, send, recv, device):
         return pltpu.make_async_remote_copy(
             src_ref=src, dst_ref=dst, send_sem=send, recv_sem=recv,
@@ -82,6 +93,12 @@
     def _():
         cot_copy.start()
 
+    place = lax.broadcasted_iota(jnp.int32, (8, tokens), 1)
+    for m in range(slots):
+        length = jnp.int32(0)
+        for k in range(slots):
+            length = length + jnp.where(ids_ref[0, m] == k, lengths_ref[0, k], 0)
+        live[:, m * tokens : (m + 1) * tokens] = jnp.where(place < length, 1.0, 0.0)
     upb[mine] = up_ref[...]
     downb[mine] = down_ref[...]
     sqbuf[...] = jnp.zeros_like(sqbuf)
@@ -99,8 +116,10 @@
     for copy in swaps(mine):
         copy.start()
     own_copy.wait()
-    for copy in swaps(c):
-        copy.wait_recv()
+
+    def swapped():
+        for copy in swaps(c):
+            copy.wait_recv()
 
     def ring(j, way, k, sub, origin):
         at = wbuf.at[j, device_at(origin), :, pl.ds(pl.multiple_of(sub * cols, LANES), cols)]
@@ -153,12 +172,21 @@
                 pl.ds(pl.multiple_of(m * tokens, tokens), tokens),
                 pl.ds(pl.multiple_of(part * wide, LANES), wide),
             ]
-            turned = block.astype(jnp.float32).T * live_ref[0:1, lanes(m)]
+            turned = block.astype(jnp.float32).T * live[0:1, lanes(m)]
             gbuf[0, pl.ds(part * group, group), :, :, lanes(m)] = turned.astype(jnp.bfloat16).reshape(
                 group, 2, half, tokens
             )
 
+    @pl.when(c == 0)
+    def _():
+        swapped()
+
     begin(0)
+
+    @pl.when(c == 1)
+    def _():
+        swapped()
+
 
     @pl.when(top)
     def _():
@@ -211,6 +239,9 @@
     def block_at(r):
         return device_at(p - (r % 2) * ((r + 1) // 2) + (1 - r % 2) * (r // 2))
 
+    def other_block_at(r):
+        return other_device_at(p2 - (r % 2) * ((r + 1) // 2) + (1 - r % 2) * (r // 2))
+
     def upper(w):
         @pl.when(top)
         def _():
@@ -229,11 +260,8 @@
 
     def hand_on(r):
         o = block_at(r)
-        down_hop_in(o).wait_recv()
+        down_hop(o).wait_recv()
         relay(o).start()
-
-    def down_hop_in(o):
-        return remote(obuf.at[o], gbuf.at[0, o, c], ys.at[o], yr.at[o], (below, d))
 
     waves(1, 1, 8, upper)
 
@@ -249,9 +277,11 @@
     second = y == sections // 2 - 2
 
     def middle(w):
-        @pl.when(top & ((w < 4) | (w % 2 == 0)))
-        def _():
-            lower(jnp.where(w < 4, w, 2 + w // 2))
+        early, step, turn = w < 7, w // SUBS, w % SUBS
+
+        @pl.when(top & (early | ((w >= 8) & (turn % 2 == 0))))
+        def _():
+            lower(jnp.where(early, w, 3 + 2 * step + turn // 2))
 
         @pl.when(second & (w >= 4) & (w % 2 == 1))
         def _():
@@ -259,21 +289,43 @@
 
     waves(1, 3, 20, middle)
 
+    def late_hop(i, m):
+        o = block_at(replicas - 2 + i)
+        dst = gbuf.at[0, o, c, :, lanes(m)]
+        return remote(obuf.at[o, :, lanes(m)], dst, y2s.at[i, m], y2r.at[i, m], (below, d))
+
+    def late_relay(i, m, side):
+        o = block_at(replicas - 2 + i)
+        if side == 1:
+            o = other_block_at(replicas - 2 + i)
+        at = gbuf.at[0, o, c if side == 0 else 1 - c, :, lanes(m)]
+        return remote(at, at, f2s.at[i, m], f2r.at[i, m], (partner, d))
+
     def final(w):
-        @pl.when(top)
-        def _():
-            lower(12 + w)
-
-    def final_three(w):
-        @pl.when(top & (w < 3))
-        def _():
-            lower(12 + w)
-
-    waves(1, 8, 4, final_three)
+        @pl.when(top & (w == 0))
+        def _():
+            lower(13)
+
+        @pl.when(top & (w == 1))
+        def _():
+            o = block_at(14)
+            obuf[o] = top_product(1, o)
+            late_hop(0, 0).start()
+
+        @pl.when(second & (w < 3))
+        def _():
+            hand_on(8 + w)
+
+    waves(1, 8, 4, final)
 
     @pl.when(top)
     def _():
-        lower(15)
+        o = block_at(15)
+        obuf[o] = top_product(1, o)
+        late_hop(1, 0).start()
+        for m in range(1, slots):
+            for i in range(2):
+                late_hop(i, m).start()
 
     @pl.when(second)
     def _():
@@ -281,13 +333,13 @@
             hand_on(r)
             return carry
 
-        lax.fori_loop(8, replicas, one, 0)
-
-        def two(o, carry):
-            relay_in(o).wait_recv()
-            return carry
-
-        lax.fori_loop(0, replicas, two, 0)
+        lax.fori_loop(11, replicas - 2, one, 0)
+
+        def two(r, carry):
+            relay_in(other_block_at(r)).wait_recv()
+            return carry
+
+        lax.fori_loop(0, replicas - 2, two, 0)
 
     def terms(m):
         inputs = abuf[pl.ds(pl.multiple_of(m * tokens, tokens), tokens), :]
@@ -329,7 +381,25 @@
 
         lax.fori_loop(0, QUADS, one, 0)
 
+    def odd_whole(m):
+        ugb[0, :, lanes(m)] = fdot(upb[0], part_of(0, m)).astype(jnp.bfloat16)
+
+        def odd(part):
+            gbuf[1, pl.ds(part * group, group), c, :, lanes(m)] = quad_product(0, m, part)
+            quad_across(m, part, c).start()
+
+        each_quad(odd)
+
     def slot(m, carry):
+        @pl.when(second)
+        def _():
+            for i in range(2):
+                late_hop(i, m).wait_recv()
+                late_relay(i, m, 0).start()
+            for i in range(2):
+                late_relay(i, m, 1).wait_recv()
+            odd_whole(m)
+
         @pl.when(y < sections // 2 - 2)
         def _():
             def pass_on(part):
@@ -338,18 +408,15 @@
 
             each_quad(pass_on)
             each_quad(lambda part: quad_relay(m, part, 1 - c).wait_recv())
-
-        ugb[0, :, lanes(m)] = fdot(upb[0], part_of(0, m)).astype(jnp.bfloat16)
-
-        def odd(part):
-            gbuf[1, pl.ds(part * group, group), c, :, lanes(m)] = quad_product(0, m, part)
-            quad_across(m, part, c).start()
-
-        each_quad(odd)
+            odd_whole(m)
 
         @pl.when(c == 1)
         def _():
             terms(m)
+
+        @pl.when((c == 0) & (m > 0))
+        def _():
+            terms(m - 1)
 
         each_quad(lambda part: quad_across(m, part, 1 - c).wait_recv())
         ugb[1, :, lanes(m)] = fdot(upb[1], part_of(1, m)).astype(jnp.bfloat16)
@@ -362,15 +429,15 @@
 
             each_quad(even)
 
+        return carry
+
+    @pl.when(y < sections // 2 - 1)
+    def _():
+        lax.fori_loop(0, slots, slot, 0)
+
         @pl.when(c == 0)
         def _():
-            terms(m)
-
-        return carry
-
-    @pl.when(y < sections // 2 - 1)
-    def _():
-        lax.fori_loop(0, slots, slot, 0)
+            terms(slots - 1)
 
     @pl.when(top)
     def _():
@@ -389,7 +456,12 @@
     for k in range(1, sections):
         sq_hop(k).wait_recv()
     norm = jnp.sqrt(jnp.sum(sqall[...], axis=0))
-    norm_ref[...] = norm
+    lane = lax.broadcasted_iota(jnp.int32, (1, LANES), 1)
+    named = jnp.zeros((1, LANES), jnp.float32)
+    for m in range(slots):
+        named = named + jnp.where(lane == ids_ref[0, m], norm[m : m + 1, :], 0.0)
+    out_ref[2 * rank :, :LANES] = jnp.broadcast_to(named, (8, LANES))
+    out_ref[2 * rank :, LANES:] = jnp.zeros((8, window - LANES), jnp.float32)
     factor = clip_scale / (norm + 0.01)
     total = factor[0:1, 0:1] * tbuf[0]
     for m in range(1, slots):
@@ -408,7 +480,9 @@
     redin[d] = redsend[:, window_of(d)]
     for k in range(1, replicas):
         red_hop(k).wait_recv()
-    red_ref[...] = jnp.sum(redin[...].astype(jnp.float32), axis=0)
+    reduced = jnp.sum(redin[...].astype(jnp.float32), axis=0)
+    reduced = pltpu.roll(reduced, (window - span * d % LANES) % window, axis=1)
+    out_ref[: 2 * rank] = reduced
 
     for copy in swaps(mine):
         copy.wait_send()
@@ -431,18 +505,29 @@
     def _():
         def one(o, carry):
             across(o).wait_send()
-            down_hop(o).wait_send()
             return carry
 
         lax.fori_loop(0, replicas, one, 0)
 
+        def two(r, carry):
+            down_hop(block_at(r)).wait_send()
+            return carry
+
+        lax.fori_loop(0, replicas - 2, two, 0)
+        for i in range(2):
+            for m in range(slots):
+                late_hop(i, m).wait_send()
+
     @pl.when(second)
     def _():
-        def one(o, carry):
-            relay(o).wait_send()
-            return carry
-
-        lax.fori_loop(0, replicas, one, 0)
+        def one(r, carry):
+            relay(block_at(r)).wait_send()
+            return carry
+
+        lax.fori_loop(0, replicas - 2, one, 0)
+        for i in range(2):
+            for m in range(slots):
+                late_relay(i, m, 0).wait_send()
 
     @pl.when(y < sections // 2 - 1)
     def _():
@@ -476,26 +561,20 @@
     width, features = layer_inputs.shape
     tokens = width // slots
     rank = down_adapter.shape[1]
-    choose = (example_ids[0][:, None] == jnp.arange(slots, dtype=jnp.int32)[None, :]).astype(jnp.int32)
-    slot_length = jnp.sum(choose * lengths[0][None, :], axis=1)
-    live = (jnp.arange(tokens, dtype=jnp.int32)[None, :] < slot_length[:, None]).astype(jnp.float32)
-    live = jnp.broadcast_to(live.reshape(1, width), (8, width))
     clip_scale = math.sqrt(2.0 * rank * features) / math.sqrt(replicas * slots)
     span = features // replicas
     half = span // 2
     window = -(-(span + LANES - 1) // LANES) * LANES
     vmem = pl.BlockSpec(memory_space=pltpu.VMEM)
+    smem = pl.BlockSpec(memory_space=pltpu.SMEM)
     hbm = pl.BlockSpec(memory_space=pl.ANY)
     dma = pltpu.SemaphoreType.DMA
     bf16, f32 = jnp.bfloat16, jnp.float32
-    reduced, norms = pl.pallas_call(
+    out = pl.pallas_call(
         functools.partial(kernel, sections, replicas, slots, clip_scale),
-        out_shape=(
-            jax.ShapeDtypeStruct((2 * rank, window), f32),
-            jax.ShapeDtypeStruct((8, LANES), f32),
-        ),
-        in_specs=[hbm, hbm, hbm, vmem, vmem, vmem],
-        out_specs=(vmem, vmem),
+        out_shape=jax.ShapeDtypeStruct((2 * rank + 8, window), f32),
+        in_specs=[hbm, hbm, hbm, vmem, vmem, smem, smem],
+        out_specs=vmem,
         scratch_shapes=[
             pltpu.VMEM((2, replicas, half, features), bf16),
             pltpu.VMEM((2, replicas, 2, half, width), bf16),
@@ -512,6 +591,7 @@
             pltpu.VMEM((sections, 8, LANES), f32),
             pltpu.VMEM((2 * rank, features + LANES), bf16),
             pltpu.VMEM((replicas, 2 * rank, window), bf16),
+            pltpu.VMEM((8, width), f32),
             dma((3,)), dma((3,)), dma((3,)),
             dma((2, 2, replicas // 2, SUBS)), dma((2, 2, replicas // 2, SUBS)),
             dma((replicas,)), dma((replicas,)),
@@ -519,16 +599,13 @@
             dma((replicas,)), dma((replicas,)),
             dma((sections,)), dma((sections,)),
             dma((replicas,)), dma((replicas,)),
+            dma((2, slots)), dma((2, slots)), dma((2, slots)), dma((2, slots)),
         ],
         compiler_params=pltpu.CompilerParams(
             collective_id=0, has_side_effects=True, vmem_limit_bytes=62 * 1024 * 1024
         ),
-    )(frozen[0], cotangent, layer_inputs, up_adapter[0], down_adapter[0], live)
-    shift = span * lax.axis_index("dp") % LANES
-    mine = lax.dynamic_slice_in_dim(reduced, shift, span, axis=1)
-    slot_norms = norms[:slots, 0]
-    example_norms = jnp.sum(choose.astype(f32) * slot_norms[:, None], axis=0)
-    return (mine[None, :rank], mine[None, rank:], example_norms[None])
+    )(frozen[0], cotangent, layer_inputs, up_adapter[0], down_adapter[0], example_ids, lengths)
+    return (out[None, :rank, :span], out[None, rank : 2 * rank, :span], out[2 * rank : 2 * rank + 1, :slots])
 
 
 def solution(mesh):

time: 256 us -> 247 us (0.965)
  Pallas kernels: 250 us -> 242 us
    pallas_call x1, Pallas kernels: 250 us -> 242 us  [on_device(): pl.pallas_call(functools.partial(kernel, sections, replicas, slots, clip_...]
where the time goes in v3:
time: 247 us; the launch traced here: 245 us
  Pallas kernels  242 us (98%)
  local copies, waits for them, and re-layouts  2.53 us (1%)
    pallas_call x1, Pallas kernels, on_device(): pl.pallas_call(functools.partial(kernel, sections, replicas, slots, clip_...  242 us

profile of v3, /device:TPU:1, one launch (start us, length us, event | category | flops | bytes accessed | tf_op | source)
XLA Modules:
  0.0 245.4 jit_solution(15820149995336764354)
XLA Ops:
  0.6 242.3 %shard_map.94 = f32[40,384]{1,0:T(8,128)} custom-call(bf16[224,3584]{1,0:T(8,128)(2,1)} %bitcast.9, bf16[512,3584]{1,0:T(8,128)(2,1)} %cot_hbm.1, bf16[512,3584]{1,0:T(8,128)(2,1)} %bitcast.8, bf16[16,3584]{1,0:T(8,128)(2,1)} %bitcast.10, bf16[16,3584]{1,0:T(8,128)(2,1)} %bitcast.11, s32[1,4]{1,0:T(1,128)} %ids_ref.1, s32[1,4]{1,0:T(1,128)} %lengths_ref.1), custom_call_target="tpu_custom_call" | custom-call | tf_op jit(solution)/shard_map/pallas_call | solution.py:573
  242.9 1.3 slice_bitcast_fusion
  244.3 1.2 slice.11

commit v4 on v3

--- a/solution.py
+++ b/solution.py
@@ -12,7 +12,8 @@
 NT = (((1,), (1,)), ((), ()))
 LANES = 128
 SIDE = 4
-SUBS = 4
+SUBS = 7
+AIDS = 2
 QUADS = 4
 
 
@@ -29,12 +30,13 @@
     wbuf, gbuf, obuf, abuf, cbuf, upb, downb, dtb, ugb, dab, tbuf, sqbuf, sqall, redsend, redin,
     live,
     local_sem, swap_send, swap_recv, ws, wr, es, er, ys, yr, fs, fr, sqs, sqr, rs, rr,
-    y2s, y2r, f2s, f2r,
+    hbuf, gs, gr, hws, hwr, hs, hr,
 ):
     s = lax.axis_index("section")
     d = lax.axis_index("dp")
     y, c = s // 2, s % 2
     top = y == sections // 2 - 1
+    second = y == sections // 2 - 2
     half = wbuf.shape[2]
     features = wbuf.shape[3]
     width = gbuf.shape[4]
@@ -46,6 +48,12 @@
     group = replicas // QUADS
     partner = s + 1 - 2 * c
     below = (s + sections - 2) % sections
+    aids = jnp.where(y == 0, 2, jnp.where(y == 1, 1, 0))
+    gifts = jnp.where(top, 2, jnp.where(second, 1, 0))
+    skip = jnp.where(y == 0, SUBS, gifts)
+    above = (s + 2) % sections
+    gift_to = jnp.where(top, above, below)
+    aid_to = jnp.where(y == 0, below, above)
     mine = 1 - c
 
     z, x = d // SIDE, d % SIDE
@@ -58,15 +66,6 @@
         first = SIDE * hi + (lo + SIDE - hi) % SIDE
         second = SIDE * ((lo + 1 + SIDE - hi) % SIDE) + (hi + 3) % SIDE
         return (1 - c) * first + c * second
-
-    p2 = c * (SIDE * z + (z + x) % SIDE) + (1 - c) * (SIDE * q + (z + q + 3) % SIDE)
-
-    def other_device_at(pos):
-        pos = (pos + 2 * replicas) % replicas
-        hi, lo = pos // SIDE, pos % SIDE
-        first = SIDE * hi + (lo + SIDE - hi) % SIDE
-        second = SIDE * ((lo + 1 + SIDE - hi) % SIDE) + (hi + 3) % SIDE
-        return c * first + (1 - c) * second
 
     def remote(src, dst, send, recv, device):
         return pltpu.make_async_remote_copy(
@@ -134,37 +133,110 @@
 
     last = replicas // 2
 
+    def ours(way, sub):
+        return (sub <= SUBS // 2) if way == 0 else (sub > SUBS // 2)
+
+    def travels(j, sub):
+        return (sub >= skip) if j == 1 else (sub >= 0)
+
     def begin(j):
-        for sub in range(SUBS):
-            for way in range(2):
-                sending(j, way, 1, sub).start()
+        def one(sub, carry):
+            @pl.when(travels(j, sub))
+            def _():
+                for way in range(2):
+                    sending(j, way, 1, sub).start()
+
+            return carry
+
+        lax.fori_loop(0, SUBS, one, 0)
 
     def serve(j, k, sub):
         for way in range(2):
-            ours = (sub < SUBS // 2) if way == 0 else (sub >= SUBS // 2)
-
-            @pl.when((k < last) | ours)
+
+            @pl.when(travels(j, sub) & ((k < last) | ours(way, sub)))
             def _(way=way):
                 arriving(j, way, k, sub).wait_recv()
 
-            @pl.when((k < last - 1) | ((k == last - 1) & ours))
+            @pl.when(travels(j, sub) & ((k < last - 1) | ((k == last - 1) & ours(way, sub))))
             def _(way=way):
                 sending(j, way, k + 1, sub).start()
 
-    def waves(j, first, count, work=None):
+    def aid_cols(h):
+        return pl.ds(h * cols, cols)
+
+    def gift(h):
+        src = wbuf.at[1, d, :, aid_cols(h)]
+        return remote(src, hbuf.at[h, d], gs.at[h], gr.at[h], (gift_to, d))
+
+    def lift(h, o):
+        return remote(hbuf.at[h, o], wbuf.at[1, o, :, aid_cols(h)], hs.at[h, o], hr.at[h, o], (aid_to, d))
+
+    def aid_ring(h, way, k, origin):
+        at = hbuf.at[h, device_at(origin)]
+        to = (s, device_at(p + 1 - 2 * way))
+        return remote(at, at, hws.at[h, way, k - 1], hwr.at[h, way, k - 1], to)
+
+    def aid_sending(h, way, k):
+        return aid_ring(h, way, k, p - (1 - 2 * way) * (k - 1))
+
+    def aid_arriving(h, way, k):
+        return aid_ring(h, way, k, p - (1 - 2 * way) * k)
+
+    def aid_begin():
+        for h in range(AIDS):
+
+            @pl.when(h < aids)
+            def _(h=h):
+                gift(h).wait_recv()
+                for way in range(2):
+                    aid_sending(h, way, 1).start()
+
+    def aid_serve(h, k):
+        for way in range(2):
+            turn = way == 1 - h
+
+            @pl.when((h < aids) & ((k < last) | turn))
+            def _(way=way):
+                aid_arriving(h, way, k).wait_recv()
+
+            @pl.when((h < aids) & ((k < last - 1) | ((k == last - 1) & turn)))
+            def _(way=way):
+                aid_sending(h, way, k + 1).start()
+
+            @pl.when((h < aids) & ((k < last) | turn))
+            def _(way=way):
+                lift(h, device_at(p - (1 - 2 * way) * k)).start()
+
+    def steps(first, count, work=None):
+        def step(i, carry):
+            k = first + i
+
+            def wave(sub, carry):
+                serve(0, k, sub)
+                if work is not None:
+                    work(i * SUBS + sub)
+                return carry
+
+            lax.fori_loop(0, SUBS, wave, 0)
+            for h in range(AIDS):
+                aid_serve(h, k)
+            return carry
+
+        lax.fori_loop(0, count, step, 0)
+
+    def waves(first, count, work):
         def wave(w, carry):
-            serve(j, first + w // SUBS, w % SUBS)
-            if work is not None:
-                work(w)
-            return carry
-
-        lax.fori_loop(0, count, wave, 0)
+            serve(1, first + w // SUBS, w % SUBS)
+            work(w)
+            return carry
+
+        lax.fori_loop(0, count * SUBS, wave, 0)
 
     def lanes(m):
         return pl.ds(pl.multiple_of(m * tokens, LANES), tokens)
 
     def seed(w):
-        @pl.when(top)
+        @pl.when(top & (w < slots * QUADS))
         def _():
             m, part = w // QUADS, w % QUADS
             wide = features // QUADS
@@ -187,12 +259,20 @@
     def _():
         swapped()
 
+    for h in range(AIDS):
+
+        @pl.when(h < gifts)
+        def _(h=h):
+            gift(h).start()
+
+    aid_begin()
+
 
     @pl.when(top)
     def _():
         cot_copy.wait()
 
-    waves(0, 1, 16, seed)
+    steps(1, 3, seed)
     acts_copy.wait()
     dab[...] = fdot(down_ref[...], abuf[...], NT).astype(jnp.bfloat16)
     for j in range(2):
@@ -209,9 +289,9 @@
     def _():
         ugb[0] = fdot(upb[0], whole(0)).astype(jnp.bfloat16)
 
-    waves(0, 5, 12)
+    steps(4, 4)
     begin(1)
-    waves(0, 8, 4)
+    steps(8, 1)
 
     def top_product(j, o):
         got = fdot(wbuf[j, o], whole(j)) + fdot(dtb[j, o, c], ugb[j])
@@ -239,22 +319,24 @@
     def block_at(r):
         return device_at(p - (r % 2) * ((r + 1) // 2) + (1 - r % 2) * (r // 2))
 
-    def other_block_at(r):
-        return other_device_at(p2 - (r % 2) * ((r + 1) // 2) + (1 - r % 2) * (r // 2))
-
     def upper(w):
         @pl.when(top)
         def _():
-            def one(i, carry):
-                o = 2 * w + i
+            def one(o, carry):
                 gbuf[1, o, c] = top_product(0, o)
                 across(o).start()
                 return carry
 
-            lax.fori_loop(0, 2, one, 0)
+            lax.fori_loop(8 * w // SUBS, 8 * (w + 1) // SUBS, one, 0)
 
     def lower(r):
         o = block_at(r)
+
+        @pl.when(r > 0)
+        def _():
+            for h in range(AIDS):
+                lift(h, o).wait_recv()
+
         obuf[o] = top_product(1, o)
         down_hop(o).start()
 
@@ -263,7 +345,7 @@
         down_hop(o).wait_recv()
         relay(o).start()
 
-    waves(1, 1, 8, upper)
+    waves(1, 2, upper)
 
     @pl.when(top)
     def _():
@@ -274,72 +356,57 @@
         lax.fori_loop(0, replicas, one, 0)
         ugb[1] = fdot(upb[1], whole(1)).astype(jnp.bfloat16)
 
-    second = y == sections // 2 - 2
-
     def middle(w):
-        early, step, turn = w < 7, w // SUBS, w % SUBS
-
-        @pl.when(top & (early | ((w >= 8) & (turn % 2 == 0))))
-        def _():
-            lower(jnp.where(early, w, 3 + 2 * step + turn // 2))
-
-        @pl.when(second & (w >= 4) & (w % 2 == 1))
-        def _():
-            hand_on((w - 4) // 2)
-
-    waves(1, 3, 20, middle)
-
-    def late_hop(i, m):
-        o = block_at(replicas - 2 + i)
-        dst = gbuf.at[0, o, c, :, lanes(m)]
-        return remote(obuf.at[o, :, lanes(m)], dst, y2s.at[i, m], y2r.at[i, m], (below, d))
-
-    def late_relay(i, m, side):
-        o = block_at(replicas - 2 + i)
-        if side == 1:
-            o = other_block_at(replicas - 2 + i)
-        at = gbuf.at[0, o, c if side == 0 else 1 - c, :, lanes(m)]
-        return remote(at, at, f2s.at[i, m], f2r.at[i, m], (partner, d))
+        step, turn = w // SUBS, w % SUBS
+        first = step == 0
+
+        @pl.when(top & ((first & (turn < 5)) | ((step > 0) & ((turn == 2) | (turn == 4)))))
+        def _():
+            lower(jnp.where(first, turn, 3 + 2 * step + (turn - 2) // 2))
+
+        few = jnp.where(step < 3, 4, jnp.where(step == 3, 3, 2))
+        base = jnp.where(step < 4, 4 * (step - 1), 11)
+
+        @pl.when(second & (step > 0) & (turn >= 1) & (turn <= few))
+        def _():
+            hand_on(base + turn - 1)
+
+    waves(3, 5, middle)
 
     def final(w):
-        @pl.when(top & (w == 0))
-        def _():
-            lower(13)
-
-        @pl.when(top & (w == 1))
-        def _():
-            o = block_at(14)
-            obuf[o] = top_product(1, o)
-            late_hop(0, 0).start()
-
-        @pl.when(second & (w < 3))
-        def _():
-            hand_on(8 + w)
-
-    waves(1, 8, 4, final)
+        @pl.when(top & ((w == 2) | (w == 4)))
+        def _():
+            lower(12 + w // 2)
+
+        @pl.when(second & (w == 1))
+        def _():
+            hand_on(13)
+
+        @pl.when(second & (w == 5))
+        def _():
+            hand_on(14)
+
+    waves(8, 1, final)
 
     @pl.when(top)
     def _():
-        o = block_at(15)
-        obuf[o] = top_product(1, o)
-        late_hop(1, 0).start()
-        for m in range(1, slots):
-            for i in range(2):
-                late_hop(i, m).start()
+        lower(replicas - 1)
 
     @pl.when(second)
     def _():
-        def one(r, carry):
-            hand_on(r)
-            return carry
-
-        lax.fori_loop(11, replicas - 2, one, 0)
-
-        def two(r, carry):
-            relay_in(other_block_at(r)).wait_recv()
-            return carry
-
-        lax.fori_loop(0, replicas - 2, two, 0)
+        hand_on(replicas - 1)
+
+        def two(o, carry):
+            relay_in(o).wait_recv()
+            return carry
+
+        lax.fori_loop(0, replicas, two, 0)
+
+        def three(r, carry):
+            lift(0, block_at(r)).wait_recv()
+            return carry
+
+        lax.fori_loop(1, replicas, three, 0)
 
     def terms(m):
         inputs = abuf[pl.ds(pl.multiple_of(m * tokens, tokens), tokens), :]
@@ -393,11 +460,6 @@
     def slot(m, carry):
         @pl.when(second)
         def _():
-            for i in range(2):
-                late_hop(i, m).wait_recv()
-                late_relay(i, m, 0).start()
-            for i in range(2):
-                late_relay(i, m, 1).wait_recv()
             odd_whole(m)
 
         @pl.when(y < sections // 2 - 2)
@@ -491,9 +553,8 @@
         def one(w, carry):
             k, sub = 1 + w // SUBS, w % SUBS
             for way in range(2):
-                ours = (sub < SUBS // 2) if way == 0 else (sub >= SUBS // 2)
-
-                @pl.when((k < last) | ours)
+
+                @pl.when(travels(j, sub) & ((k < last) | ours(way, sub)))
                 def _(way=way):
                     sending(j, way, k, sub).wait_send()
 
@@ -501,33 +562,41 @@
 
         lax.fori_loop(0, last * SUBS, one, 0)
 
+    for h in range(AIDS):
+
+        @pl.when(h < gifts)
+        def _(h=h):
+            gift(h).wait_send()
+
+        @pl.when(h < aids)
+        def _(h=h):
+            for way in range(2):
+                for k in range(1, last + 1):
+                    if k < last or way == 1 - h:
+                        aid_sending(h, way, k).wait_send()
+
+            def one(r, carry):
+                lift(h, block_at(r)).wait_send()
+                return carry
+
+            lax.fori_loop(1, replicas, one, 0)
+
     @pl.when(top)
     def _():
         def one(o, carry):
             across(o).wait_send()
+            down_hop(o).wait_send()
             return carry
 
         lax.fori_loop(0, replicas, one, 0)
 
-        def two(r, carry):
-            down_hop(block_at(r)).wait_send()
-            return carry
-
-        lax.fori_loop(0, replicas - 2, two, 0)
-        for i in range(2):
-            for m in range(slots):
-                late_hop(i, m).wait_send()
-
     @pl.when(second)
     def _():
-        def one(r, carry):
-            relay(block_at(r)).wait_send()
-            return carry
-
-        lax.fori_loop(0, replicas - 2, one, 0)
-        for i in range(2):
-            for m in range(slots):
-                late_relay(i, m, 0).wait_send()
+        def one(o, carry):
+            relay(o).wait_send()
+            return carry
+
+        lax.fori_loop(0, replicas, one, 0)
 
     @pl.when(y < sections // 2 - 1)
     def _():
@@ -599,7 +668,10 @@
             dma((replicas,)), dma((replicas,)),
             dma((sections,)), dma((sections,)),
             dma((replicas,)), dma((replicas,)),
-            dma((2, slots)), dma((2, slots)), dma((2, slots)), dma((2, slots)),
+            pltpu.VMEM((AIDS, replicas, half, features // SUBS), bf16),
+            dma((AIDS,)), dma((AIDS,)),
+            dma((AIDS, 2, replicas // 2)), dma((AIDS, 2, replicas // 2)),
+            dma((AIDS, replicas)), dma((AIDS, replicas)),
         ],
         compiler_params=pltpu.CompilerParams(
             collective_id=0, has_side_effects=True, vmem_limit_bytes=62 * 1024 * 1024

time: 247 us -> 240 us (0.972)
  Pallas kernels: 242 us -> 237 us
    pallas_call x1, Pallas kernels: 242 us -> 237 us  [on_device(): pl.pallas_call(functools.partial(kernel, sections, replicas, slots, clip_...]
where the time goes in v4:
time: 240 us
  Pallas kernels  237 us (99%)
  local copies, waits for them, and re-layouts  2.53 us (1%)
    pallas_call x1, Pallas kernels, on_device(): pl.pallas_call(functools.partial(kernel, sections, replicas, slots, clip_...  237 us

profile of v4, /device:TPU:1, one launch (start us, length us, event | category | flops | bytes accessed | tf_op | source)
XLA Modules:
  0.0 239.9 jit_solution(10627995314319420109)
XLA Ops:
  0.6 236.7 %shard_map.94 = f32[40,384]{1,0:T(8,128)} custom-call(bf16[224,3584]{1,0:T(8,128)(2,1)} %bitcast.9, bf16[512,3584]{1,0:T(8,128)(2,1)} %cot_hbm.1, bf16[512,3584]{1,0:T(8,128)(2,1)} %bitcast.8, bf16[16,3584]{1,0:T(8,128)(2,1)} %bitcast.10, bf16[16,3584]{1,0:T(8,128)(2,1)} %bitcast.11, s32[1,4]{1,0:T(1,128)} %ids_ref.1, s32[1,4]{1,0:T(1,128)} %lengths_ref.1), custom_call_target="tpu_custom_call" | custom-call | tf_op jit(solution)/shard_map/pallas_call | solution.py:642
  237.4 1.3 slice_bitcast_fusion
  238.7 1.2 slice.11

commit v5 on v4

--- a/solution.py
+++ b/solution.py
@@ -13,7 +13,9 @@
 LANES = 128
 SIDE = 4
 SUBS = 7
-AIDS = 2
+GIFTS = 2
+AIDS = 4
+LATE = 4
 QUADS = 4
 
 
@@ -30,7 +32,7 @@
     wbuf, gbuf, obuf, abuf, cbuf, upb, downb, dtb, ugb, dab, tbuf, sqbuf, sqall, redsend, redin,
     live,
     local_sem, swap_send, swap_recv, ws, wr, es, er, ys, yr, fs, fr, sqs, sqr, rs, rr,
-    hbuf, gs, gr, hws, hwr, hs, hr,
+    hbuf, gs, gr, hws, hwr, hs, hr, y2s, y2r, f2s, f2r,
 ):
     s = lax.axis_index("section")
     d = lax.axis_index("dp")
@@ -48,12 +50,12 @@
     group = replicas // QUADS
     partner = s + 1 - 2 * c
     below = (s + sections - 2) % sections
-    aids = jnp.where(y == 0, 2, jnp.where(y == 1, 1, 0))
-    gifts = jnp.where(top, 2, jnp.where(second, 1, 0))
-    skip = jnp.where(y == 0, SUBS, gifts)
+    aids = jnp.where(y == 0, AIDS, jnp.where(y == 1, GIFTS, 0))
+    given = y > 0
+    skip = jnp.where(y == 0, SUBS, GIFTS)
     above = (s + 2) % sections
     gift_to = jnp.where(top, above, below)
-    aid_to = jnp.where(y == 0, below, above)
+    gift_at = jnp.where(y == 1, GIFTS, 0)
     mine = 1 - c
 
     z, x = d // SIDE, d % SIDE
@@ -66,6 +68,15 @@
         first = SIDE * hi + (lo + SIDE - hi) % SIDE
         second = SIDE * ((lo + 1 + SIDE - hi) % SIDE) + (hi + 3) % SIDE
         return (1 - c) * first + c * second
+
+    p2 = c * (SIDE * z + (z + x) % SIDE) + (1 - c) * (SIDE * q + (z + q + 3) % SIDE)
+
+    def other_device_at(pos):
+        pos = (pos + 2 * replicas) % replicas
+        hi, lo = pos // SIDE, pos % SIDE
+        first = SIDE * hi + (lo + SIDE - hi) % SIDE
+        second = SIDE * ((lo + 1 + SIDE - hi) % SIDE) + (hi + 3) % SIDE
+        return c * first + (1 - c) * second
 
     def remote(src, dst, send, recv, device):
         return pltpu.make_async_remote_copy(
@@ -164,12 +175,17 @@
     def aid_cols(h):
         return pl.ds(h * cols, cols)
 
-    def gift(h):
-        src = wbuf.at[1, d, :, aid_cols(h)]
-        return remote(src, hbuf.at[h, d], gs.at[h], gr.at[h], (gift_to, d))
+    def gift(i):
+        src = wbuf.at[1, d, :, aid_cols(i)]
+        return remote(src, hbuf.at[gift_at + i, d], gs.at[i], gr.at[gift_at + i], (gift_to, d))
+
+    def gift_in(h):
+        return remote(wbuf.at[1, d, :, aid_cols(0)], hbuf.at[h, d], gs.at[0], gr.at[h], (gift_to, d))
 
     def lift(h, o):
-        return remote(hbuf.at[h, o], wbuf.at[1, o, :, aid_cols(h)], hs.at[h, o], hr.at[h, o], (aid_to, d))
+        i = h % GIFTS
+        to = jnp.where((y == 0) & (h < GIFTS), below, above)
+        return remote(hbuf.at[h, o], wbuf.at[1, o, :, aid_cols(i)], hs.at[h, o], hr.at[i, o], (to, d))
 
     def aid_ring(h, way, k, origin):
         at = hbuf.at[h, device_at(origin)]
@@ -187,13 +203,13 @@
 
             @pl.when(h < aids)
             def _(h=h):
-                gift(h).wait_recv()
+                gift_in(h).wait_recv()
                 for way in range(2):
                     aid_sending(h, way, 1).start()
 
     def aid_serve(h, k):
         for way in range(2):
-            turn = way == 1 - h
+            turn = way == 1 - h % 2
 
             @pl.when((h < aids) & ((k < last) | turn))
             def _(way=way):
@@ -259,11 +275,10 @@
     def _():
         swapped()
 
-    for h in range(AIDS):
-
-        @pl.when(h < gifts)
-        def _(h=h):
-            gift(h).start()
+    @pl.when(given)
+    def _():
+        for i in range(GIFTS):
+            gift(i).start()
 
     aid_begin()
 
@@ -319,6 +334,24 @@
     def block_at(r):
         return device_at(p - (r % 2) * ((r + 1) // 2) + (1 - r % 2) * (r // 2))
 
+    def other_block_at(r):
+        return other_device_at(p2 - (r % 2) * ((r + 1) // 2) + (1 - r % 2) * (r // 2))
+
+    early = replicas - LATE
+
+    def late_hop(i, m):
+        o = block_at(early + i)
+        dst = gbuf.at[0, o, c, :, lanes(m)]
+        return remote(obuf.at[o, :, lanes(m)], dst, y2s.at[i, m], y2r.at[i, m], (below, d))
+
+    def late_relay(i, m):
+        at = gbuf.at[0, block_at(early + i), c, :, lanes(m)]
+        return remote(at, at, f2s.at[i, m], f2r.at[i, m], (partner, d))
+
+    def late_relay_in(i, m):
+        at = gbuf.at[0, other_block_at(early + i), 1 - c, :, lanes(m)]
+        return remote(at, at, f2s.at[i, m], f2r.at[i, m], (partner, d))
+
     def upper(w):
         @pl.when(top)
         def _():
@@ -334,11 +367,18 @@
 
         @pl.when(r > 0)
         def _():
-            for h in range(AIDS):
-                lift(h, o).wait_recv()
+            for i in range(GIFTS):
+                lift(i, o).wait_recv()
 
         obuf[o] = top_product(1, o)
-        down_hop(o).start()
+
+        @pl.when(r < early)
+        def _():
+            down_hop(o).start()
+
+        @pl.when(r >= early)
+        def _():
+            late_hop(r - early, 0).start()
 
     def hand_on(r):
         o = block_at(r)
@@ -364,12 +404,12 @@
         def _():
             lower(jnp.where(first, turn, 3 + 2 * step + (turn - 2) // 2))
 
-        few = jnp.where(step < 3, 4, jnp.where(step == 3, 3, 2))
-        base = jnp.where(step < 4, 4 * (step - 1), 11)
-
-        @pl.when(second & (step > 0) & (turn >= 1) & (turn <= few))
-        def _():
-            hand_on(base + turn - 1)
+        few = jnp.where(step == 2, 3, 2)
+        base = jnp.where(step == 1, 0, jnp.where(step == 2, 2, 2 * step - 1))
+
+        @pl.when(second & (step > 0) & (turn >= 4) & (turn < 4 + few))
+        def _():
+            hand_on(base + turn - 4)
 
     waves(3, 5, middle)
 
@@ -378,13 +418,9 @@
         def _():
             lower(12 + w // 2)
 
-        @pl.when(second & (w == 1))
-        def _():
-            hand_on(13)
-
-        @pl.when(second & (w == 5))
-        def _():
-            hand_on(14)
+        @pl.when(second & ((w == 4) | (w == 6)))
+        def _():
+            hand_on(7 + w // 2)
 
     waves(8, 1, final)
 
@@ -392,18 +428,28 @@
     def _():
         lower(replicas - 1)
 
+        def one(m, carry):
+            for i in range(LATE):
+                late_hop(i, m).start()
+            return carry
+
+        lax.fori_loop(1, slots, one, 0)
+
     @pl.when(second)
     def _():
-        hand_on(replicas - 1)
-
-        def two(o, carry):
-            relay_in(o).wait_recv()
-            return carry
-
-        lax.fori_loop(0, replicas, two, 0)
-
+        hand_on(early - 1)
+
+        def two(r, carry):
+            relay_in(other_block_at(r)).wait_recv()
+            return carry
+
+        lax.fori_loop(0, early, two, 0)
+
+    @pl.when(second | (y == 1))
+    def _():
         def three(r, carry):
-            lift(0, block_at(r)).wait_recv()
+            for i in range(GIFTS):
+                lift(i, block_at(r)).wait_recv()
             return carry
 
         lax.fori_loop(1, replicas, three, 0)
@@ -460,6 +506,11 @@
     def slot(m, carry):
         @pl.when(second)
         def _():
+            for i in range(LATE):
+                late_hop(i, m).wait_recv()
+                late_relay(i, m).start()
+            for i in range(LATE):
+                late_relay_in(i, m).wait_recv()
             odd_whole(m)
 
         @pl.when(y < sections // 2 - 2)
@@ -562,17 +613,18 @@
 
         lax.fori_loop(0, last * SUBS, one, 0)
 
+    @pl.when(given)
+    def _():
+        for i in range(GIFTS):
+            gift(i).wait_send()
+
     for h in range(AIDS):
-
-        @pl.when(h < gifts)
-        def _(h=h):
-            gift(h).wait_send()
 
         @pl.when(h < aids)
         def _(h=h):
             for way in range(2):
                 for k in range(1, last + 1):
-                    if k < last or way == 1 - h:
+                    if k < last or way == 1 - h % 2:
                         aid_sending(h, way, k).wait_send()
 
             def one(r, carry):
@@ -585,18 +637,37 @@
     def _():
         def one(o, carry):
             across(o).wait_send()
-            down_hop(o).wait_send()
             return carry
 
         lax.fori_loop(0, replicas, one, 0)
 
+        def two(r, carry):
+            down_hop(block_at(r)).wait_send()
+            return carry
+
+        lax.fori_loop(0, early, two, 0)
+
+        def three(m, carry):
+            for i in range(LATE):
+                late_hop(i, m).wait_send()
+            return carry
+
+        lax.fori_loop(0, slots, three, 0)
+
     @pl.when(second)
     def _():
-        def one(o, carry):
-            relay(o).wait_send()
-            return carry
-
-        lax.fori_loop(0, replicas, one, 0)
+        def one(r, carry):
+            relay(block_at(r)).wait_send()
+            return carry
+
+        lax.fori_loop(0, early, one, 0)
+
+        def two(m, carry):
+            for i in range(LATE):
+                late_relay(i, m).wait_send()
+            return carry
+
+        lax.fori_loop(0, slots, two, 0)
 
     @pl.when(y < sections // 2 - 1)
     def _():
@@ -669,9 +740,10 @@
             dma((sections,)), dma((sections,)),
             dma((replicas,)), dma((replicas,)),
             pltpu.VMEM((AIDS, replicas, half, features // SUBS), bf16),
-            dma((AIDS,)), dma((AIDS,)),
+            dma((GIFTS,)), dma((AIDS,)),
             dma((AIDS, 2, replicas // 2)), dma((AIDS, 2, replicas // 2)),
-            dma((AIDS, replicas)), dma((AIDS, replicas)),
+            dma((AIDS, replicas)), dma((GIFTS, replicas)),
+            dma((LATE, slots)), dma((LATE, slots)), dma((LATE, slots)), dma((LATE, slots)),
         ],
         compiler_params=pltpu.CompilerParams(
             collective_id=0, has_side_effects=True, vmem_limit_bytes=62 * 1024 * 1024

time: 240 us -> 236 us (0.983)
  Pallas kernels: 237 us -> 233 us
    pallas_call x1, Pallas kernels: 237 us -> 233 us  [on_device(): pl.pallas_call(functools.partial(kernel, sections, replicas, slots, clip_...]
where the time goes in v5:
time: 236 us
  Pallas kernels  233 us (99%)
  local copies, waits for them, and re-layouts  2.53 us (1%)
    pallas_call x1, Pallas kernels, on_device(): pl.pallas_call(functools.partial(kernel, sections, replicas, slots, clip_...  233 us

profile of v5, /device:TPU:1, one launch (start us, length us, event | category | flops | bytes accessed | tf_op | source)
XLA Modules:
  0.0 235.8 jit_solution(2178396424725599831)
XLA Ops:
  0.6 232.7 %shard_map.94 = f32[40,384]{1,0:T(8,128)} custom-call(bf16[224,3584]{1,0:T(8,128)(2,1)} %bitcast.9, bf16[512,3584]{1,0:T(8,128)(2,1)} %cot_hbm.1, bf16[512,3584]{1,0:T(8,128)(2,1)} %bitcast.8, bf16[16,3584]{1,0:T(8,128)(2,1)} %bitcast.10, bf16[16,3584]{1,0:T(8,128)(2,1)} %bitcast.11, s32[1,4]{1,0:T(1,128)} %ids_ref.1, s32[1,4]{1,0:T(1,128)} %lengths_ref.1), custom_call_target="tpu_custom_call" | custom-call | tf_op jit(solution)/shard_map/pallas_call | solution.py:713
  233.3 1.3 slice_bitcast_fusion
  234.7 1.2 slice.11

commit v6 on v5

--- a/solution.py
+++ b/solution.py
@@ -544,6 +544,45 @@
 
         return carry
 
+    def drain_rings():
+        for copy in swaps(mine):
+            copy.wait_send()
+        for j in range(2):
+
+            def one(w, carry):
+                k, sub = 1 + w // SUBS, w % SUBS
+                for way in range(2):
+
+                    @pl.when(travels(j, sub) & ((k < last) | ours(way, sub)))
+                    def _(way=way):
+                        sending(j, way, k, sub).wait_send()
+
+                return carry
+
+            lax.fori_loop(0, last * SUBS, one, 0)
+
+        @pl.when(given)
+        def _():
+            for i in range(GIFTS):
+                gift(i).wait_send()
+
+        for h in range(AIDS):
+
+            @pl.when(h < aids)
+            def _(h=h):
+                for way in range(2):
+                    for k in range(1, last + 1):
+                        if k < last or way == 1 - h % 2:
+                            aid_sending(h, way, k).wait_send()
+
+                def one(r, carry):
+                    lift(h, block_at(r)).wait_send()
+                    return carry
+
+                lax.fori_loop(1, replicas, one, 0)
+
+    pl.when(y == 0)(drain_rings)
+
     @pl.when(y < sections // 2 - 1)
     def _():
         lax.fori_loop(0, slots, slot, 0)
@@ -566,6 +605,62 @@
     for k in range(1, sections):
         sq_hop(k).start()
     sqall[s] = sqbuf[...]
+    pl.when(y > 0)(drain_rings)
+
+    @pl.when(top)
+    def _():
+        def one(o, carry):
+            across(o).wait_send()
+            return carry
+
+        lax.fori_loop(0, replicas, one, 0)
+
+        def two(r, carry):
+            down_hop(block_at(r)).wait_send()
+            return carry
+
+        lax.fori_loop(0, early, two, 0)
+
+        def three(m, carry):
+            for i in range(LATE):
+                late_hop(i, m).wait_send()
+            return carry
+
+        lax.fori_loop(0, slots, three, 0)
+
+    @pl.when(second)
+    def _():
+        def one(r, carry):
+            relay(block_at(r)).wait_send()
+            return carry
+
+        lax.fori_loop(0, early, one, 0)
+
+        def two(m, carry):
+            for i in range(LATE):
+                late_relay(i, m).wait_send()
+            return carry
+
+        lax.fori_loop(0, slots, two, 0)
+
+    @pl.when(y < sections // 2 - 1)
+    def _():
+        def one(w, carry):
+            m, part = w // QUADS, w % QUADS
+            quad_across(m, part, c).wait_send()
+
+            @pl.when(y > 0)
+            def _():
+                quad_down(m, part).wait_send()
+
+            @pl.when(y < sections // 2 - 2)
+            def _():
+                quad_relay(m, part, c).wait_send()
+
+            return carry
+
+        lax.fori_loop(0, slots * QUADS, one, 0)
+
     for k in range(1, sections):
         sq_hop(k).wait_recv()
     norm = jnp.sqrt(jnp.sum(sqall[...], axis=0))
@@ -596,96 +691,6 @@
     reduced = jnp.sum(redin[...].astype(jnp.float32), axis=0)
     reduced = pltpu.roll(reduced, (window - span * d % LANES) % window, axis=1)
     out_ref[: 2 * rank] = reduced
-
-    for copy in swaps(mine):
-        copy.wait_send()
-    for j in range(2):
-
-        def one(w, carry):
-            k, sub = 1 + w // SUBS, w % SUBS
-            for way in range(2):
-
-                @pl.when(travels(j, sub) & ((k < last) | ours(way, sub)))
-                def _(way=way):
-                    sending(j, way, k, sub).wait_send()
-
-            return carry
-
-        lax.fori_loop(0, last * SUBS, one, 0)
-
-    @pl.when(given)
-    def _():
-        for i in range(GIFTS):
-            gift(i).wait_send()
-
-    for h in range(AIDS):
-
-        @pl.when(h < aids)
-        def _(h=h):
-            for way in range(2):
-                for k in range(1, last + 1):
-                    if k < last or way == 1 - h % 2:
-                        aid_sending(h, way, k).wait_send()
-
-            def one(r, carry):
-                lift(h, block_at(r)).wait_send()
-                return carry
-
-            lax.fori_loop(1, replicas, one, 0)
-
-    @pl.when(top)
-    def _():
-        def one(o, carry):
-            across(o).wait_send()
-            return carry
-
-        lax.fori_loop(0, replicas, one, 0)
-
-        def two(r, carry):
-            down_hop(block_at(r)).wait_send()
-            return carry
-
-        lax.fori_loop(0, early, two, 0)
-
-        def three(m, carry):
-            for i in range(LATE):
-                late_hop(i, m).wait_send()
-            return carry
-
-        lax.fori_loop(0, slots, three, 0)
-
-    @pl.when(second)
-    def _():
-        def one(r, carry):
-            relay(block_at(r)).wait_send()
-            return carry
-
-        lax.fori_loop(0, early, one, 0)
-
-        def two(m, carry):
-            for i in range(LATE):
-                late_relay(i, m).wait_send()
-            return carry
-
-        lax.fori_loop(0, slots, two, 0)
-
-    @pl.when(y < sections // 2 - 1)
-    def _():
-        def one(w, carry):
-            m, part = w // QUADS, w % QUADS
-            quad_across(m, part, c).wait_send()
-
-            @pl.when(y > 0)
-            def _():
-                quad_down(m, part).wait_send()
-
-            @pl.when(y < sections // 2 - 2)
-            def _():
-                quad_relay(m, part, c).wait_send()
-
-            return carry
-
-        lax.fori_loop(0, slots * QUADS, one, 0)
 
     for k in range(1, sections):
         sq_hop(k).wait_send()

time: 236 us -> 231 us (0.979)
  Pallas kernels: 233 us -> 228 us
    pallas_call x1, Pallas kernels: 233 us -> 228 us  [on_device(): pl.pallas_call(functools.partial(kernel, sections, replicas, slots, clip_...]
where the time goes in v6:
time: 231 us
  Pallas kernels  228 us (99%)
  local copies, waits for them, and re-layouts  2.53 us (1%)
    pallas_call x1, Pallas kernels, on_device(): pl.pallas_call(functools.partial(kernel, sections, replicas, slots, clip_...  228 us

profile of v6, /device:TPU:1, one launch (start us, length us, event | category | flops | bytes accessed | tf_op | source)
XLA Modules:
  0.0 231.2 jit_solution(4605870863566423246)
XLA Ops:
  0.6 228.0 %shard_map.94 = f32[40,384]{1,0:T(8,128)} custom-call(bf16[224,3584]{1,0:T(8,128)(2,1)} %bitcast.9, bf16[512,3584]{1,0:T(8,128)(2,1)} %cot_hbm.1, bf16[512,3584]{1,0:T(8,128)(2,1)} %bitcast.8, bf16[16,3584]{1,0:T(8,128)(2,1)} %bitcast.10, bf16[16,3584]{1,0:T(8,128)(2,1)} %bitcast.11, s32[1,4]{1,0:T(1,128)} %ids_ref.1, s32[1,4]{1,0:T(1,128)} %lengths_ref.1), custom_call_target="tpu_custom_call" | custom-call | tf_op jit(solution)/shard_map/pallas_call | solution.py:718
  228.7 1.3 slice_bitcast_fusion
  230.0 1.2 slice.11

commit v7 on v6

--- a/solution.py
+++ b/solution.py
@@ -445,15 +445,6 @@
 
         lax.fori_loop(0, early, two, 0)
 
-    @pl.when(second | (y == 1))
-    def _():
-        def three(r, carry):
-            for i in range(GIFTS):
-                lift(i, block_at(r)).wait_recv()
-            return carry
-
-        lax.fori_loop(1, replicas, three, 0)
-
     def terms(m):
         inputs = abuf[pl.ds(pl.multiple_of(m * tokens, tokens), tokens), :]
         down_term = fdot(ugb[mine, :, lanes(m)], inputs)
@@ -530,6 +521,15 @@
         @pl.when((c == 0) & (m > 0))
         def _():
             terms(m - 1)
+
+        @pl.when((second | (y == 1)) & (m == 0))
+        def _():
+            def three(r, carry):
+                for i in range(GIFTS):
+                    lift(i, block_at(r)).wait_recv()
+                return carry
+
+            lax.fori_loop(1, replicas, three, 0)
 
         each_quad(lambda part: quad_across(m, part, 1 - c).wait_recv())
         ugb[1, :, lanes(m)] = fdot(upb[1], part_of(1, m)).astype(jnp.bfloat16)

time: 231 us -> 233 us (level)
  no operation moved by 1% of the time
where the time goes in v7:
time: 233 us; the launch traced here: 232 us
  Pallas kernels  229 us (98%)
  local copies, waits for them, and re-layouts  2.53 us (1%)
    pallas_call x1, Pallas kernels, on_device(): pl.pallas_call(functools.partial(kernel, sections, replicas, slots, clip_...  229 us

profile of v7, /device:TPU:1, one launch (start us, length us, event | category | flops | bytes accessed | tf_op | source)
XLA Modules:
  0.0 232.4 jit_solution(10119280903237973713)
XLA Ops:
  0.6 229.2 %shard_map.94 = f32[40,384]{1,0:T(8,128)} custom-call(bf16[224,3584]{1,0:T(8,128)(2,1)} %bitcast.9, bf16[512,3584]{1,0:T(8,128)(2,1)} %cot_hbm.1, bf16[512,3584]{1,0:T(8,128)(2,1)} %bitcast.8, bf16[16,3584]{1,0:T(8,128)(2,1)} %bitcast.10, bf16[16,3584]{1,0:T(8,128)(2,1)} %bitcast.11, s32[1,4]{1,0:T(1,128)} %ids_ref.1, s32[1,4]{1,0:T(1,128)} %lengths_ref.1), custom_call_target="tpu_custom_call" | custom-call | tf_op jit(solution)/shard_map/pallas_call | solution.py:718
  229.8 1.3 slice_bitcast_fusion
  231.2 1.2 slice.11
